TPU v7x, 32 devices: a whole 2x2x4 slice. The times are simulated.
32 devices in a mesh: scan: 16 (over z, x, core), tile: 2 (over y).
Axes of the slice: x: 2, y: 2, z: 4, core: 2. Of those that a mesh axis runs over, the one named last changes fastest.
Arguments:
- probe_modes: float32 [12, 2, 128, 128], replicated, may hold values from -5 to 5
- patterns: float32 [128, 128, 128], P(('scan', 'tile')), may hold values from 0.005 to 300
- specimen: float32 [2, 2048, 512], P(None, 'scan', 'tile'), may hold values from -17.5 to 17.5
- offsets: int32 [128, 2], P(('scan', 'tile')), may hold values from -128 to 2048, as said below
Outputs:
- new_probe: float32 [12, 2, 128, 128], replicated
- new_specimen: float32 [2, 2048, 512], P(None, 'scan', 'tile')
Inputs may be any that keep to these rules, and one draw needn't show every extreme that they name: `offsets`: position p lies in aligned block b = p // 4, held by the device of scan index s = b // (the number of tile devices) and tile index t = b % (the number of tile devices); its row offset lies in s * 128 - 128 to s * 128 + 128, its column offset in t * 256 - 128 to t * 256 + 256, both ends included; in every block one position has its row offset at the lower end and its column offset at the upper end, and one has its row offset at the upper end.
All inputs are finite; a program needn't handle non-finite values.
Results may differ from a plain program's by a relative error of at most 0.0001.
Values sent between devices are 32-bit elements; how exact they have to be, the bound alone decides.
A program may use at most 64 MiB of HBM per device.

v0:
```python
import math

import jax
import jax.numpy as jnp
import numpy as np
from jax import lax
from jax.experimental import pallas as pl
from jax.experimental.pallas import tpu as pltpu
from jax.sharding import PartitionSpec as P

NS_STEPS = 8


highest = lax.Precision.HIGHEST
light_floor = 0.05
object_reg = 0.5
probe_reg = 1.0
total_eps = 1e-06


def dft_tables(detector):
    indices = np.arange(detector, dtype=np.int64)
    angles = -2.0 * np.pi / detector * (indices[:, None] * indices[None, :] % detector)
    table_re = np.cos(angles) / np.sqrt(detector)
    table_im = np.sin(angles) / np.sqrt(detector)
    right = np.block([[table_re, table_im], [-table_im, table_re]]).astype(np.float32)
    left = np.ascontiguousarray(right.T)
    parts = []
    for table in (right, left):
        high = table.astype(jnp.bfloat16)
        low = (table - high.astype(np.float32)).astype(jnp.bfloat16)
        parts.append((high, low))
    (rh, rl), (lh, ll) = parts
    return (
        np.concatenate([rh, rl, rh], axis=0),
        np.concatenate([lh, ll, lh], axis=1),
        np.concatenate([rh, rl, rh], axis=1),
        np.concatenate([lh, ll, lh], axis=0),
    )


def halves(value):
    high = value.astype(jnp.bfloat16)
    low = (value - high.astype(jnp.float32)).astype(jnp.bfloat16)
    return high, low


def scan_kernel(
    offs, probe, patterns, extended, right_f, left_f, left_b, right_b,
    packed, frame_out,
    ext, frame, deep, half, far, power, grad, light,
    *, block_rows, block_cols,
):
    modes = probe.shape[0]
    det = probe.shape[-1]
    count = patterns.shape[0]
    col_blocks = extended.shape[2] // det
    f32 = jnp.float32
    row_base = lax.axis_index("scan") * block_rows - det
    col_base = lax.axis_index("tile") * block_cols - det
    lanes = lax.broadcasted_iota(jnp.int32, (det, det), 1)
    for c in range(2):
        for j in range(col_blocks):
            ext[c, j] = extended[c, :, j * det : (j + 1) * det]
        ext[c, col_blocks] = jnp.zeros_like(ext[c, col_blocks])
    frame[...] = jnp.zeros_like(frame)
    grad[...] = jnp.zeros_like(grad)
    light[...] = jnp.zeros_like(light)
    acc = jnp.zeros((det, det), f32)
    for k in range(modes):
        acc = acc + probe[k, 0] * probe[k, 0] + probe[k, 1] * probe[k, 1]
    power[...] = acc

    def one(p, total):
        row = offs[p, 0] - row_base
        col = offs[p, 1] - col_base
        block = col // det
        shift = col - block * det
        back = lax.rem(det - shift, det)
        rows = pl.ds(row, det)

        def patch_part(c):
            first = pltpu.roll(ext[c, block, rows, :], back, 1)
            second = pltpu.roll(ext[c, block + 1, rows, :], back, 1)
            return jnp.where(lanes < det - shift, first, second)

        patch_re = patch_part(0)
        patch_im = patch_part(1)
        patch_light = patch_re * patch_re + patch_im * patch_im
        light[...] = light[...] + patch_light
        total = total + patch_light * power[...]
        for k in range(modes):
            at = pl.ds(k * det, det)
            pr, pi = probe[k, 0], probe[k, 1]
            for c, value in enumerate((pr * patch_re - pi * patch_im, pr * patch_im + pi * patch_re)):
                high, low = halves(value)
                deep[at, pl.ds(c * det, det)] = high
                deep[at, pl.ds((2 + c) * det, det)] = high
                deep[at, pl.ds((4 + c) * det, det)] = low
        half[...] = jnp.dot(deep[...], right_f[...], preferred_element_type=f32)
        model = jnp.zeros((det, det), f32)
        for k in range(0, modes, 2):
            lo_at, hi_at = pl.ds(k * det, det), pl.ds((k + 1) * det, det)
            first, second = half[lo_at, :], half[hi_at, :]
            paired = jnp.concatenate(
                [
                    jnp.concatenate([first[:, :det], second[:, :det]], axis=1),
                    jnp.concatenate([first[:, det:], second[:, det:]], axis=1),
                ],
                axis=0,
            )
            high, low = halves(paired)
            stacked = jnp.concatenate([high, high, low], axis=0)
            out = jnp.dot(left_f[...], stacked, preferred_element_type=f32)
            far[:, pl.ds(k * det, 2 * det)] = out
            squares = out * out
            both = squares[:det] + squares[det:]
            model = model + both[:, :det] + both[:, det:]
        factor = jnp.sqrt(patterns[p]) / jnp.sqrt(jnp.maximum(model, light_floor)) - 1.0
        wide = jnp.concatenate([factor, factor], axis=1)
        wide = jnp.concatenate([wide, wide], axis=0)
        for k in range(0, modes, 2):
            high, low = halves(far[:, pl.ds(k * det, 2 * det)] * wide)
            stacked = jnp.concatenate([high, high, low], axis=0)
            out = jnp.dot(left_b[...], stacked, preferred_element_type=f32)
            high, low = halves(out)
            for m in range(2):
                at = pl.ds((k + m) * det, det)
                for c in range(2):
                    part_h = high[c * det : (c + 1) * det, m * det : (m + 1) * det]
                    part_l = low[c * det : (c + 1) * det, m * det : (m + 1) * det]
                    deep[at, pl.ds(c * det, det)] = part_h
                    deep[at, pl.ds((2 + c) * det, det)] = part_h
                    deep[at, pl.ds((4 + c) * det, det)] = part_l
        half[...] = jnp.dot(deep[...], right_b[...], preferred_element_type=f32)
        num_re = jnp.zeros((det, det), f32)
        num_im = jnp.zeros((det, det), f32)
        for k in range(modes):
            at = pl.ds(k * det, det)
            cr, ci = half[at, :det], half[at, det:]
            pr, pi = probe[k, 0], probe[k, 1]
            grad[0, k] = grad[0, k] + patch_re * cr + patch_im * ci
            grad[1, k] = grad[1, k] + patch_re * ci - patch_im * cr
            num_re = num_re + pr * cr + pi * ci
            num_im = num_im + pr * ci - pi * cr
        zero = jnp.zeros((det, det), f32)
        for c, value in enumerate((num_re, num_im, power[...])):
            turned = pltpu.roll(value, shift, 1)
            frame[c, block, rows, :] = frame[c, block, rows, :] + jnp.where(lanes >= shift, turned, zero)
            frame[c, block + 1, rows, :] = frame[c, block + 1, rows, :] + jnp.where(lanes < shift, turned, zero)
        return total

    model_grid = lax.fori_loop(0, count, one, jnp.zeros((det, det), f32))
    measured = jnp.zeros((det, det), f32)
    for p in range(count):
        measured = measured + patterns[p]
    tiles = det // 8
    for k in range(2 * modes):
        packed[k * tiles : (k + 1) * tiles] = grad[k // modes, k % modes].reshape(tiles, 8, det)
    last = 2 * modes * tiles
    packed[last : last + tiles] = light[...].reshape(tiles, 8, det)
    packed[last + tiles] = jnp.sum(measured.reshape(tiles, 8, det), axis=0)
    packed[last + tiles + 1] = jnp.sum(model_grid.reshape(tiles, 8, det), axis=0)
    for extra in range(last + tiles + 2, packed.shape[0]):
        packed[extra] = jnp.zeros((8, det), f32)
    for c in range(3):
        for j in range(col_blocks):
            frame_out[c, :, j * det : (j + 1) * det] = frame[c, j]


def scan_positions(offsets, probe_modes, patterns, extended, block_rows, block_cols):
    modes, _, det, _ = probe_modes.shape
    f32 = jnp.float32
    ext_rows, ext_cols = extended.shape[1:]
    col_blocks = ext_cols // det
    vmem = pl.BlockSpec(memory_space=pltpu.VMEM)
    tables = [jnp.asarray(t) for t in dft_tables(det)]

    def kernel(*refs):
        scan_kernel(*refs, block_rows=block_rows, block_cols=block_cols)

    return pl.pallas_call(
        kernel,
        name="scan_positions",
        out_shape=(
            jax.ShapeDtypeStruct((packed_tiles(modes, det), 8, det), f32),
            jax.ShapeDtypeStruct((3, ext_rows, ext_cols), f32),
        ),
        in_specs=[pl.BlockSpec(memory_space=pltpu.SMEM)] + [vmem] * 7,
        out_specs=(vmem,) * 2,
        scratch_shapes=[
            pltpu.VMEM((2, col_blocks + 1, ext_rows, det), f32),
            pltpu.VMEM((3, col_blocks + 1, ext_rows, det), f32),
            pltpu.VMEM((modes * det, 6 * det), jnp.bfloat16),
            pltpu.VMEM((modes * det, 2 * det), f32),
            pltpu.VMEM((2 * det, modes * det), f32),
            pltpu.VMEM((det, det), f32),
            pltpu.VMEM((2, modes, det, det), f32),
            pltpu.VMEM((det, det), f32),
        ],
        compiler_params=pltpu.CompilerParams(vmem_limit_bytes=48 * 1024 * 1024),
    )(offsets, probe_modes, patterns, extended, *tables)


def newton_steps(gram_re, gram_im):
    mode_count = gram_re.shape[0]
    upper = jnp.concatenate([gram_re, -gram_im], axis=1)
    lower = jnp.concatenate([gram_im, gram_re], axis=1)
    embedded = jnp.concatenate([upper, lower], axis=0)
    frobenius = jnp.sqrt(jnp.sum(embedded * embedded))
    identity = jnp.eye(2 * mode_count, dtype=jnp.float32)
    current = embedded / frobenius
    inverse = identity
    for repeat in range(NS_STEPS):
        factor = 1.5 * identity - 0.5 * jnp.dot(
            inverse, current, precision=highest, preferred_element_type=jnp.float32
        )
        current = jnp.dot(current, factor, precision=highest, preferred_element_type=jnp.float32)
        inverse = jnp.dot(factor, inverse, precision=highest, preferred_element_type=jnp.float32)
    inverse = inverse / jnp.sqrt(frobenius)
    return (inverse[:mode_count, :mode_count], inverse[mode_count:, :mode_count])


def gram_parts(mode_rows):
    real_rows = mode_rows[: mode_rows.shape[0] // 2]
    imag_rows = mode_rows[mode_rows.shape[0] // 2 :]
    gram_re = jnp.dot(
        real_rows, real_rows.T, precision=highest, preferred_element_type=jnp.float32
    ) + jnp.dot(imag_rows, imag_rows.T, precision=highest, preferred_element_type=jnp.float32)
    gram_im = jnp.dot(
        real_rows, imag_rows.T, precision=highest, preferred_element_type=jnp.float32
    ) - jnp.dot(imag_rows, real_rows.T, precision=highest, preferred_element_type=jnp.float32)
    return (gram_re, gram_im)


def orthonormal_rows(mode_rows, gram_re, gram_im, power_ratio):
    real_rows = mode_rows[: mode_rows.shape[0] // 2]
    imag_rows = mode_rows[mode_rows.shape[0] // 2 :]
    mix_re, mix_im = newton_steps(gram_re, gram_im)
    ortho_re = jnp.dot(
        mix_re.T, real_rows, precision=highest, preferred_element_type=jnp.float32
    ) - jnp.dot(mix_im.T, imag_rows, precision=highest, preferred_element_type=jnp.float32)
    ortho_im = jnp.dot(
        mix_im.T, real_rows, precision=highest, preferred_element_type=jnp.float32
    ) + jnp.dot(mix_re.T, imag_rows, precision=highest, preferred_element_type=jnp.float32)
    weight = jnp.sqrt(power_ratio * jnp.diagonal(gram_re))
    return jnp.stack([ortho_re, ortho_im], axis=1) * weight[:, None, None]


fast_bits = (("scan", 1), ("scan", 2), ("scan", 4), ("tile", 1))
halvings = 3


def packed_tiles(modes, det):
    tiles = (2 * modes + 1) * (det // 8) + 2
    step = len(fast_bits) * 2**halvings
    return -(-tiles // step) * step


def mesh_bits():
    bits = list(fast_bits)
    for axis in ("scan", "tile"):
        bit = 1
        while bit < lax.axis_size(axis):
            if (axis, bit) not in bits:
                bits.append((axis, bit))
            bit *= 2
    return bits


def directions():
    return [(i, j) for i, j in ((1, 0), (-1, 0), (0, 1), (0, -1), (1, 1), (1, -1), (-1, 1), (-1, -1))]


def exchange_kernel(bits, packed, frame, out, interior, acc, landing, *rest):
    slots = rest[:8]
    send_sem, recv_sem, fold_send, fold_recv = rest[8:]
    pieces = len(fast_bits)
    piece = packed.shape[0] // pieces
    det = (frame.shape[1] - interior.shape[1]) // 2
    block_rows, block_cols = interior.shape[1:]
    here = {axis: lax.axis_index(axis) for axis in ("scan", "tile")}
    sizes = {axis: lax.axis_size(axis) for axis in ("scan", "tile")}

    def digit(axis, bit):
        return (here[axis] // bit) % 2

    def partner(axis, bit):
        return {axis: here[axis] + bit * (1 - 2 * digit(axis, bit))}

    def copy(src, dst, g, step, axis, bit):
        return pltpu.make_async_remote_copy(
            src_ref=src, dst_ref=dst, send_sem=send_sem.at[g, step], recv_sem=recv_sem.at[g, step],
            device_id=partner(axis, bit), device_id_type=pl.DeviceIdType.MESH,
        )

    plans = []
    for g in range(pieces):
        order = [fast_bits[(g + i) % pieces] for i in range(pieces)] + bits[pieces:]
        steps = []
        start, size, land = g * piece, piece, 0
        for axis, bit in order[:halvings]:
            size //= 2
            mine = digit(axis, bit)
            keep, give = start + mine * size, start + (1 - mine) * size
            steps.append(("halve", axis, bit, give, keep, size, land))
            start = keep
            land += size
        for axis, bit in order[halvings:]:
            steps.append(("both", axis, bit, start, start, size, land))
            land += size
        for axis, bit in reversed(order[:halvings]):
            low = start - digit(axis, bit) * size
            steps.append(("gather", axis, bit, start, low + (1 - digit(axis, bit)) * size, size, land))
            start = low
            land += size
            size *= 2
        plans.append(steps)
    total = len(plans[0])

    def make(g, step):
        kind, axis, bit, give, keep, size, land = plans[g][step]
        source = packed if step == 0 else acc
        src = source.at[pl.ds(give, size)]
        return copy(src, landing.at[g, pl.ds(land, size)], g, step, axis, bit)

    def settle(g, step):
        kind, axis, bit, give, keep, size, land = plans[g][step]
        source = packed if step == 0 else acc
        arrived = landing[g, pl.ds(land, size)]
        acc[pl.ds(keep, size)] = arrived if kind == "gather" else source[pl.ds(keep, size)] + arrived

    def span(shift, block):
        low = {-1: 0, 0: det, 1: det + block}[shift]
        return pl.ds(low, block if shift == 0 else det)

    def inner(shift, block):
        low = {-1: block - det, 0: 0, 1: 0}[shift]
        return pl.ds(low, block if shift == 0 else det)

    def valid(shift_rows, shift_cols):
        row, col = here["scan"] + shift_rows, here["tile"] + shift_cols
        return (row >= 0) & (row < sizes["scan"]) & (col >= 0) & (col < sizes["tile"])

    def fold(index):
        shift_rows, shift_cols = directions()[index]
        return pltpu.make_async_remote_copy(
            src_ref=frame.at[:, span(shift_rows, block_rows), span(shift_cols, block_cols)],
            dst_ref=slots[index],
            send_sem=fold_send.at[index],
            recv_sem=fold_recv.at[index],
            device_id={
                "scan": (here["scan"] + shift_rows + sizes["scan"]) % sizes["scan"],
                "tile": (here["tile"] + shift_cols + sizes["tile"]) % sizes["tile"],
            },
            device_id_type=pl.DeviceIdType.MESH,
        )

    def fold_start(indices):
        for index in indices:
            @pl.when(valid(*directions()[index]))
            def _():
                fold(index).start()

    interior[...] = frame[:, det : det + block_rows, det : det + block_cols]
    for g in range(pieces):
        make(g, 0).start()
    fold_start((0, 1))
    for step in range(total):
        for g in range(pieces):
            make(g, step).wait()
            settle(g, step)
            if step + 1 < total:
                make(g, step + 1).start()
        if step == 0:
            fold_start((2, 3))
        if step == 1:
            fold_start((4, 5, 6, 7))
    out[...] = acc[...]
    for index, (shift_rows, shift_cols) in enumerate(directions()):
        @pl.when(valid(shift_rows, shift_cols))
        def _():
            fold(index).wait_send()

        @pl.when(valid(-shift_rows, -shift_cols))
        def _():
            fold(index).wait_recv()
            rows, cols = inner(shift_rows, block_rows), inner(shift_cols, block_cols)
            interior[:, rows, cols] = interior[:, rows, cols] + slots[index][...]


def exchange(packed, frame, det, block_rows, block_cols):
    f32 = jnp.float32
    bits = mesh_bits()
    pieces = len(fast_bits)
    piece = packed.shape[0] // pieces
    steps = len(bits) + halvings
    small = piece // 2**halvings
    land = 2 * (piece - small) + (len(bits) - halvings) * small
    vmem = pl.BlockSpec(memory_space=pltpu.VMEM)
    slots = [
        pltpu.VMEM((3, det if i else block_rows, det if j else block_cols), f32) for i, j in directions()
    ]

    def kernel(*refs):
        exchange_kernel(bits, *refs)

    return pl.pallas_call(
        kernel,
        name="exchange",
        out_shape=(
            jax.ShapeDtypeStruct(packed.shape, f32),
            jax.ShapeDtypeStruct((3, block_rows, block_cols), f32),
        ),
        in_specs=[vmem, vmem],
        out_specs=(vmem, vmem),
        scratch_shapes=[
            pltpu.VMEM(packed.shape, f32),
            pltpu.VMEM((pieces, land) + packed.shape[1:], f32),
            *slots,
            pltpu.SemaphoreType.DMA((pieces, steps)),
            pltpu.SemaphoreType.DMA((pieces, steps)),
            pltpu.SemaphoreType.DMA((8,)),
            pltpu.SemaphoreType.DMA((8,)),
        ],
        compiler_params=pltpu.CompilerParams(has_side_effects=True, vmem_limit_bytes=40 * 1024 * 1024),
    )(packed, frame)


def halo_kernel(specimen, out, *rest):
    slots = rest[:8]
    send_sem, recv_sem = rest[8:]
    block_rows, block_cols = specimen.shape[1:]
    det = (out.shape[1] - block_rows) // 2
    here = {axis: lax.axis_index(axis) for axis in ("scan", "tile")}
    sizes = {axis: lax.axis_size(axis) for axis in ("scan", "tile")}

    def edge(shift, block):
        low = {-1: 0, 0: 0, 1: block - det}[shift]
        return pl.ds(low, block if shift == 0 else det)

    def outer(shift, block):
        low = {-1: det + block, 0: det, 1: 0}[shift]
        return pl.ds(low, block if shift == 0 else det)

    def valid(shift_rows, shift_cols):
        row, col = here["scan"] + shift_rows, here["tile"] + shift_cols
        return (row >= 0) & (row < sizes["scan"]) & (col >= 0) & (col < sizes["tile"])

    def send(index):
        shift_rows, shift_cols = directions()[index]
        return pltpu.make_async_remote_copy(
            src_ref=specimen.at[:, edge(shift_rows, block_rows), edge(shift_cols, block_cols)],
            dst_ref=slots[index],
            send_sem=send_sem.at[index],
            recv_sem=recv_sem.at[index],
            device_id={
                "scan": (here["scan"] + shift_rows + sizes["scan"]) % sizes["scan"],
                "tile": (here["tile"] + shift_cols + sizes["tile"]) % sizes["tile"],
            },
            device_id_type=pl.DeviceIdType.MESH,
        )

    for index, shifts in enumerate(directions()):
        @pl.when(valid(*shifts))
        def _():
            send(index).start()
    out[...] = jnp.zeros_like(out)
    out[:, det : det + block_rows, det : det + block_cols] = specimen[...]
    for index, (shift_rows, shift_cols) in enumerate(directions()):
        @pl.when(valid(shift_rows, shift_cols))
        def _():
            send(index).wait_send()

        @pl.when(valid(-shift_rows, -shift_cols))
        def _():
            send(index).wait_recv()
            out[:, outer(shift_rows, block_rows), outer(shift_cols, block_cols)] = slots[index][...]


def with_halo(specimen, det):
    channels, block_rows, block_cols = specimen.shape
    vmem = pl.BlockSpec(memory_space=pltpu.VMEM)
    slots = [
        pltpu.VMEM((channels, det if i else block_rows, det if j else block_cols), jnp.float32)
        for i, j in directions()
    ]
    return pl.pallas_call(
        halo_kernel,
        name="halo",
        out_shape=jax.ShapeDtypeStruct((channels, block_rows + 2 * det, block_cols + 2 * det), jnp.float32),
        in_specs=[vmem],
        out_specs=vmem,
        scratch_shapes=[*slots, pltpu.SemaphoreType.DMA((8,)), pltpu.SemaphoreType.DMA((8,))],
        compiler_params=pltpu.CompilerParams(has_side_effects=True, vmem_limit_bytes=16 * 1024 * 1024),
    )(specimen)


def body(probe_modes, patterns, specimen, offsets):
    detector = probe_modes.shape[-1]
    mode_count = probe_modes.shape[0]
    block_rows = specimen.shape[1]
    block_cols = specimen.shape[2]
    extended = with_halo(specimen, detector)
    packed, frame_sum = scan_positions(
        offsets, probe_modes, patterns, extended, block_rows, block_cols
    )
    summed, interior = exchange(packed, frame_sum, detector, block_rows, block_cols)
    pixels = detector * detector
    tiles = detector // 8
    last = 2 * mode_count * tiles
    grad_total = summed[:last].reshape(2 * mode_count, pixels)
    light_total = summed[last : last + tiles].reshape(1, pixels)
    measured_all = jnp.sum(summed[last + tiles])
    model_all = jnp.sum(summed[last + tiles + 1])
    power_ratio = measured_all / (model_all + total_eps)
    new_specimen = specimen + interior[0:2] / (interior[2] + object_reg)[None]
    probe_rows = jnp.swapaxes(probe_modes, 0, 1).reshape(2 * mode_count, pixels)
    updated = probe_rows + grad_total / (light_total + probe_reg)
    gram_re, gram_im = gram_parts(updated)
    new_probe = orthonormal_rows(updated, gram_re, gram_im, power_ratio).reshape(probe_modes.shape)
    return (new_probe, new_specimen)


def solution(mesh):
    return jax.shard_map(
        body,
        mesh=mesh,
        in_specs=(
            P(),
            P(("scan", "tile"), None, None),
            P(None, "scan", "tile"),
            P(("scan", "tile"), None),
        ),
        out_specs=(P(), P(None, "scan", "tile")),
        check_vma=False,
    )
```

profile of v0, /device:TPU:0, one launch (start us, length us, event | category | flops | bytes accessed | tf_op | source)
XLA Modules:
  0.0 134.4 jit_solution(5606588082826779543)
XLA Ops:
  0.6 0.0 copy-start
  0.6 0.0 copy-start.3
  0.7 1.1 copy-done.3
  1.7 16.6 %halo.1.refs_3_ = f32[2,384,512]{2,1,0:T(8,128)S(1)} custom-call(f32[2,128,256]{2,1,0:T(8,128)S(1)} %copy-done.3), custom_call_target="tpu_custom_call" | custom-call | tf_op jit(solution)/shard_map/halo/pallas_call | solution.py:488
  18.3 0.8 copy.14.refs_0_
  19.0 0.0 copy-done
  19.0 0.0 copy-done.11
  19.1 1.0 copy-done.5
  20.0 1.0 copy-done.6
  21.0 1.0 copy-done.7
  22.0 1.0 copy-done.8
  23.0 22.0 %scan_positions.1 = (f32[416,8,128]{2,1,0:T(8,128)}, f32[3,384,512]{2,1,0:T(8,128)}) custom-call(s32[4,2]{1,0:T(4,128)S(1)} %copy.14.refs_0_, f32[12,2,128,128]{3,2,1,0:T(8,128)S(1)} %copy-done, f32[4,128,128]{2,1,0:T(8,128)S(1)} %copy-done.11, f32[2,384,512]{2,1,0:T(8,128)S(1)} %halo.1.refs_3_, bf16[768,256]{1,0:T(8,128)(2,1)S(1)} %copy-done.5, ...), custom_call_target="tpu_custom_call" | custom-call | tf_op jit(solution)/shard_map/scan_positions/pallas_call | solution.py:182
  45.0 1.7 %copy-done.1 = f32[3,384,512]{2,1,0:T(8,128)S(1)} copy-done((f32[3,384,512]{2,1,0:T(8,128)S(1)}, f32[3,384,512]{2,1,0:T(8,128)}, u32[]{:S(2)}) %copy-start.1) | copy-done | bytes 2359320
  46.7 1.5 %copy-done.2 = f32[416,8,128]{2,1,0:T(8,128)S(1)} copy-done((f32[416,8,128]{2,1,0:T(8,128)S(1)}, f32[416,8,128]{2,1,0:T(8,128)}, u32[]{:S(2)}) %copy-start.2) | copy-done | bytes 1703960
  48.1 58.6 %exchange.1 = (f32[416,8,128]{2,1,0:T(8,128)S(1)}, f32[3,128,256]{2,1,0:T(8,128)S(1)}) custom-call(f32[416,8,128]{2,1,0:T(8,128)S(1)} %copy-done.2, f32[3,384,512]{2,1,0:T(8,128)S(1)} %copy-done.1), custom_call_target="tpu_custom_call" | custom-call | tf_op jit(solution)/shard_map/exchange/pallas_call | solution.py:408
  106.8 0.0 copy-start.9
  106.8 0.7 copy-done.9
  107.5 1.2 slice.32
  108.8 2.6 %reshape.30 = f32[24,16384]{1,0:T(8,128)} reshape(f32[384,8,128]{2,1,0:T(8,128)} %slice.32) | data formatting | bytes 3145728 | tf_op jit(solution)/shard_map/reshape | solution.py:512
  111.3 0.0 copy-start.12
  111.3 0.1 copy.13
  111.5 1.3 copy-done.12
  112.7 1.0 bitcast_add_fusion
  113.7 1.4 %fusion.11 = f32[12,12]{1,0:T(8,128)S(1)} fusion(f32[24,16384]{1,0:T(8,128)S(1)} %bitcast_add_fusion), kind=kOutput, calls=%fused_computation.27 | convolution fusion | flops 28311552 | bytes 2097728 | tf_op jit(solution)/shard_map/dot_general | solution.py:230
  115.1 1.5 %fusion.28 = (f32[12,12]{1,0:T(8,128)S(1)}, f32[12,12]{1,0:T(8,128)S(1)}) fusion(f32[12,12]{1,0:T(8,128)S(1)} %fusion.11, f32[24,16384]{1,0:T(8,128)S(1)} %bitcast_add_fusion), kind=kOutput, calls=%fused_computation.57 | convolution fusion | flops 28311840 | bytes 2106496 | tf_op jit(solution)/shard_map/dot_general | solution.py:232
  116.6 1.5 %fusion.20 = f32[12,12]{1,0:T(8,128)S(1)} fusion(f32[24,16384]{1,0:T(8,128)S(1)} %bitcast_add_fusion), kind=kOutput, calls=%fused_computation.36 | convolution fusion | flops 28311552 | bytes 1049152 | tf_op jit(solution)/shard_map/dot_general | solution.py:227
  118.2 1.6 %convolution_add_fusion.1 = f32[12,12]{1,0:T(8,128)S(1)} fusion(f32[12,12]{1,0:T(8,128)S(1)} %fusion.20, f32[24,16384]{1,0:T(8,128)S(1)} %bitcast_add_fusion), kind=kOutput, calls=%fused_computation.23 | convolution fusion | flops 28311696 | bytes 1057344 | tf_op jit(solution)/shard_map/dot_general | solution.py:229
  119.8 0.7 multiply_reduce_fusion
  121.1 0.2 fusion.7
  121.4 0.2 fusion.27
  121.6 0.1 fusion.22
  121.7 0.2 fusion.6
  121.9 0.1 fusion.30
  122.0 0.1 fusion.29
  122.2 0.2 fusion.5
  122.3 0.1 fusion.32
  122.5 0.2 fusion.31
  122.6 0.2 fusion.4
  122.8 0.1 fusion.34
  122.9 0.2 fusion.33
  123.1 0.2 fusion.3
  123.3 0.1 fusion.36
  123.4 0.2 fusion.35
  123.6 0.2 fusion.2
  123.7 0.1 fusion.38
  123.9 0.1 fusion.37
  124.0 0.2 fusion.1
  124.2 0.1 fusion.40
  124.3 0.2 fusion.39
  124.5 0.2 fusion
  124.7 0.1 convolution_divide_fusion
  124.9 1.1 fusion.16
  125.9 1.0 convolution_subtract_fusion
  127.0 0.2 copy.18
  127.2 1.0 fusion.14
  128.2 1.0 convolution_add_fusion
  129.3 0.2 copy.19
  129.5 0.1 bitcast_bitcast_fusion
  129.6 0.7 gather_fusion
  130.3 0.6 slice_reduce_fusion
  132.2 0.0 copy-start.10
  132.2 0.0 copy-start.4
  132.3 1.4 %maximum_multiply_fusion = f32[12,2,128,128]{3,2,1,0:T(8,128)} fusion(f32[12,1,128,128]{3,2,1,0:T(8,128)S(1)} %get-tuple-element.14, f32[12,1,128,128]{3,2,1,0:T(8,128)S(1)} %get-tuple-element.15, f32[12]{0:T(128)S(1)} %multiply_sqrt_fusion), kind=kLoop, calls=%fused_computation.4 | loop fusion | flops 786432 | bytes 3145776 | tf_op jit(solution)/shard_map/mul | solution.py:247
  133.7 0.7 divide_add_fusion
  (13 shorter events, 0.0 us)
Async XLA Ops:
  0.6 18.4 %copy-start = (f32[12,2,128,128]{3,2,1,0:T(8,128)S(1)}, f32[12,2,128,128]{3,2,1,0:T(8,128)}, u32[]{:S(2)}) copy-start(f32[12,2,128,128]{3,2,1,0:T(8,128)} %refs_1_.1) | copy-start | bytes 4718596
  0.6 1.1 copy-start.3
  1.7 17.3 %copy-start.11 = (f32[4,128,128]{2,1,0:T(8,128)S(1)}, f32[4,128,128]{2,1,0:T(8,128)}, u32[]{:S(2)}) copy-start(f32[4,128,128]{2,1,0:T(8,128)} %refs_2_.1) | copy-start | bytes 786436
  19.0 1.0 copy-start.5
  20.0 1.0 copy-start.6
  21.0 1.0 copy-start.7
  22.0 1.0 copy-start.8
  45.0 1.7 %copy-start.1 = (f32[3,384,512]{2,1,0:T(8,128)S(1)}, f32[3,384,512]{2,1,0:T(8,128)}, u32[]{:S(2)}) copy-start(f32[3,384,512]{2,1,0:T(8,128)} %get-tuple-element.7.refs_1_) | copy-start | bytes 7077892
  46.7 1.5 %copy-start.2 = (f32[416,8,128]{2,1,0:T(8,128)S(1)}, f32[416,8,128]{2,1,0:T(8,128)}, u32[]{:S(2)}) copy-start(f32[416,8,128]{2,1,0:T(8,128)} %get-tuple-element.6.refs_0_) | copy-start | bytes 5111812
  106.8 0.7 copy-start.9
  111.3 1.4 %copy-start.12 = (f32[24,16384]{1,0:T(8,128)S(1)}, f32[24,16384]{1,0:T(8,128)}, u32[]{:S(2)}) copy-start(f32[24,16384]{1,0:T(8,128)} %reshape.30) | copy-start | bytes 4718596
  132.2 1.4 %copy-start.10 = (f32[3,128,256]{2,1,0:T(8,128)S(1)}, f32[3,128,256]{2,1,0:T(8,128)}, u32[]{:S(2)}) copy-start(f32[3,128,256]{2,1,0:T(8,128)} %copy-done.9) | copy-start | bytes 1179652
  132.2 1.4 %copy-start.4 = (f32[2,128,256]{2,1,0:T(8,128)S(1)}, f32[2,128,256]{2,1,0:T(8,128)}, u32[]{:S(2)}) copy-start(f32[2,128,256]{2,1,0:T(8,128)} %specimen.1) | copy-start | bytes 786436
where the time goes:
time: 135 us; the launch traced here: 134 us
  Pallas kernels  97.2 us (72%)
  local copies, waits for them, and re-layouts  16.1 us (12%)
  matrix products  13.8 us (10%)
  other arithmetic  4.39 us (3%)
  between operations  2.94 us (2%)
    pallas_call x1, Pallas kernels, exchange(): pl.pallas_call(kernel, name='exchange', out_shape=(jax.ShapeDtypeStruct(p...  58.6 us
    pallas_call x1, Pallas kernels, scan_positions(): pl.pallas_call(kernel, name='scan_positions', out_shape=(jax.ShapeDtypeSt...  22 us
    pallas_call x1, Pallas kernels, with_halo(): pl.pallas_call(halo_kernel, name='halo', out_shape=jax.ShapeDtypeStruct((...  16.6 us
    unnamed x29, local copies, waits for them, and re-layouts  11.4 us

commit v1 on v0

--- a/solution.py
+++ b/solution.py
@@ -47,10 +47,11 @@
 
 def scan_kernel(
     offs, probe, patterns, extended, right_f, left_f, left_b, right_b,
-    packed, frame_out,
+    packed_a, packed_b, packed_c, totals, frame_out,
     ext, frame, deep, half, far, power, grad, light,
     *, block_rows, block_cols,
 ):
+    packed = (packed_a, packed_b, packed_c)
     modes = probe.shape[0]
     det = probe.shape[-1]
     count = patterns.shape[0]
@@ -154,15 +155,9 @@
     measured = jnp.zeros((det, det), f32)
     for p in range(count):
         measured = measured + patterns[p]
-    tiles = det // 8
-    for k in range(2 * modes):
-        packed[k * tiles : (k + 1) * tiles] = grad[k // modes, k % modes].reshape(tiles, 8, det)
-    last = 2 * modes * tiles
-    packed[last : last + tiles] = light[...].reshape(tiles, 8, det)
-    packed[last + tiles] = jnp.sum(measured.reshape(tiles, 8, det), axis=0)
-    packed[last + tiles + 1] = jnp.sum(model_grid.reshape(tiles, 8, det), axis=0)
-    for extra in range(last + tiles + 2, packed.shape[0]):
-        packed[extra] = jnp.zeros((8, det), f32)
+    pack_gradient(packed, grad, light)
+    totals[0] = jnp.sum(measured.reshape(det // 8, 8, det), axis=0)
+    totals[1] = jnp.sum(model_grid.reshape(det // 8, 8, det), axis=0)
     for c in range(3):
         for j in range(col_blocks):
             frame_out[c, :, j * det : (j + 1) * det] = frame[c, j]
@@ -183,11 +178,12 @@
         kernel,
         name="scan_positions",
         out_shape=(
-            jax.ShapeDtypeStruct((packed_tiles(modes, det), 8, det), f32),
+            *[jax.ShapeDtypeStruct((2,) + shape, f32) for shape in group_shapes(modes, det)],
+            jax.ShapeDtypeStruct((2, 8, det), f32),
             jax.ShapeDtypeStruct((3, ext_rows, ext_cols), f32),
         ),
         in_specs=[pl.BlockSpec(memory_space=pltpu.SMEM)] + [vmem] * 7,
-        out_specs=(vmem,) * 2,
+        out_specs=(vmem,) * 5,
         scratch_shapes=[
             pltpu.VMEM((2, col_blocks + 1, ext_rows, det), f32),
             pltpu.VMEM((3, col_blocks + 1, ext_rows, det), f32),
@@ -202,133 +198,140 @@
     )(offsets, probe_modes, patterns, extended, *tables)
 
 
-def newton_steps(gram_re, gram_im):
-    mode_count = gram_re.shape[0]
-    upper = jnp.concatenate([gram_re, -gram_im], axis=1)
-    lower = jnp.concatenate([gram_im, gram_re], axis=1)
-    embedded = jnp.concatenate([upper, lower], axis=0)
-    frobenius = jnp.sqrt(jnp.sum(embedded * embedded))
-    identity = jnp.eye(2 * mode_count, dtype=jnp.float32)
-    current = embedded / frobenius
-    inverse = identity
-    for repeat in range(NS_STEPS):
-        factor = 1.5 * identity - 0.5 * jnp.dot(
-            inverse, current, precision=highest, preferred_element_type=jnp.float32
-        )
-        current = jnp.dot(current, factor, precision=highest, preferred_element_type=jnp.float32)
-        inverse = jnp.dot(factor, inverse, precision=highest, preferred_element_type=jnp.float32)
-    inverse = inverse / jnp.sqrt(frobenius)
-    return (inverse[:mode_count, :mode_count], inverse[mode_count:, :mode_count])
-
-
-def gram_parts(mode_rows):
-    real_rows = mode_rows[: mode_rows.shape[0] // 2]
-    imag_rows = mode_rows[mode_rows.shape[0] // 2 :]
-    gram_re = jnp.dot(
-        real_rows, real_rows.T, precision=highest, preferred_element_type=jnp.float32
-    ) + jnp.dot(imag_rows, imag_rows.T, precision=highest, preferred_element_type=jnp.float32)
-    gram_im = jnp.dot(
-        real_rows, imag_rows.T, precision=highest, preferred_element_type=jnp.float32
-    ) - jnp.dot(imag_rows, real_rows.T, precision=highest, preferred_element_type=jnp.float32)
-    return (gram_re, gram_im)
-
-
-def orthonormal_rows(mode_rows, gram_re, gram_im, power_ratio):
-    real_rows = mode_rows[: mode_rows.shape[0] // 2]
-    imag_rows = mode_rows[mode_rows.shape[0] // 2 :]
-    mix_re, mix_im = newton_steps(gram_re, gram_im)
-    ortho_re = jnp.dot(
-        mix_re.T, real_rows, precision=highest, preferred_element_type=jnp.float32
-    ) - jnp.dot(mix_im.T, imag_rows, precision=highest, preferred_element_type=jnp.float32)
-    ortho_im = jnp.dot(
-        mix_im.T, real_rows, precision=highest, preferred_element_type=jnp.float32
-    ) + jnp.dot(mix_re.T, imag_rows, precision=highest, preferred_element_type=jnp.float32)
-    weight = jnp.sqrt(power_ratio * jnp.diagonal(gram_re))
-    return jnp.stack([ortho_re, ortho_im], axis=1) * weight[:, None, None]
-
-
-fast_bits = (("scan", 1), ("scan", 2), ("scan", 4), ("tile", 1))
-halvings = 3
-
-
-def packed_tiles(modes, det):
-    tiles = (2 * modes + 1) * (det // 8) + 2
-    step = len(fast_bits) * 2**halvings
-    return -(-tiles // step) * step
-
-
-def mesh_bits():
-    bits = list(fast_bits)
-    for axis in ("scan", "tile"):
-        bit = 1
+core_dim = ("scan", 1, 2)
+slab_dims = (("scan", 2, 2), ("tile", 1, 2), ("scan", 4, 4))
+slab_orders = ((0, 1, 2), (1, 2, 0), (2, 0, 1))
+slab_count = math.prod(size for _, _, size in slab_dims)
+
+
+def extra_bits():
+    bits = []
+    for axis, bit in (("scan", 16), ("tile", 2)):
         while bit < lax.axis_size(axis):
-            if (axis, bit) not in bits:
-                bits.append((axis, bit))
+            bits.append((axis, bit, 2))
             bit *= 2
     return bits
 
 
+def group_modes(modes):
+    return modes // (2 * len(slab_orders))
+
+
+def group_shapes(modes, det):
+    shapes = []
+    for q, order in enumerate(slab_orders):
+        planes = 2 * group_modes(modes) + (q == len(slab_orders) - 1)
+        shapes.append(tuple(slab_dims[i][2] for i in order) + (planes, det // slab_count, det))
+    return shapes
+
+
+def slab_coords(tile):
+    coords = []
+    for _, _, size in reversed(slab_dims):
+        coords.append(tile % size)
+        tile = tile // size
+    return coords[::-1]
+
+
+def plane_of(half, q, i, modes):
+    per = group_modes(modes)
+    return half * (modes // 2) + q * per + i // 2, i % 2
+
+
+def pack_gradient(packed, grad, light):
+    modes, det = grad.shape[1], grad.shape[-1]
+    rows = det // slab_count
+    for tile in range(slab_count):
+        at = slice(tile * rows, (tile + 1) * rows)
+        coords = slab_coords(tile)
+        for q, order in enumerate(slab_orders):
+            spot = tuple(coords[i] for i in order)
+            for half in range(2):
+                for i in range(2 * group_modes(modes)):
+                    k, c = plane_of(half, q, i, modes)
+                    packed[q][(half,) + spot + (i,)] = grad[c, k, at, :]
+                if q == len(slab_orders) - 1:
+                    packed[q][(half,) + spot + (2 * group_modes(modes),)] = light[at, :]
+
+
 def directions():
     return [(i, j) for i, j in ((1, 0), (-1, 0), (0, 1), (0, -1), (1, 1), (1, -1), (-1, 1), (-1, -1))]
 
 
-def exchange_kernel(bits, packed, frame, out, interior, acc, landing, *rest):
-    slots = rest[:8]
-    send_sem, recv_sem, fold_send, fold_recv = rest[8:]
-    pieces = len(fast_bits)
-    piece = packed.shape[0] // pieces
-    det = (frame.shape[1] - interior.shape[1]) // 2
-    block_rows, block_cols = interior.shape[1:]
+def digit(dim):
+    axis, bit, size = dim
+    return (lax.axis_index(axis) // bit) % size
+
+
+def flipped(value, size, d):
+    if size == 2:
+        return 1 - value if d else value
+    low, high = value % 2, value // 2
+    low = 1 - low if d % 2 else low
+    high = 1 - high if d // 2 else high
+    return low + 2 * high
+
+
+def peer(moves):
+    where = {}
+    for dim, d in moves:
+        axis, bit, size = dim
+        here = digit(dim)
+        base = where.get(axis, lax.axis_index(axis))
+        where[axis] = base + bit * (flipped(here, size, d) - here)
+    return where
+
+
+def full_dot(a, b):
+    return jnp.dot(a, b, precision=highest, preferred_element_type=jnp.float32)
+
+
+def finish_kernel(extra, *refs):
+    groups = len(slab_orders)
+    packed, refs = refs[:groups], refs[groups:]
+    totals, frame, probe, specimen, new_probe, new_specimen, *refs = refs
+    land0, refs = refs[:groups], refs[groups:]
+    acc, refs = refs[:groups], refs[groups:]
+    land = []
+    for step in range(3):
+        land.append(refs[:groups])
+        refs = refs[groups:]
+    landx, refs = refs[:groups], refs[groups:]
+    full, refs = refs[:groups], refs[groups:]
+    slots, refs = refs[:8], refs[8:]
+    total_land, gram_out, gram_land, gram_x, interior, send_sem, recv_sem, fold_send, fold_recv = refs
+    f32 = jnp.float32
+    modes, det = probe.shape[0], probe.shape[-1]
+    per = 2 * group_modes(modes)
+    rows = det // slab_count
+    planes = 2 * modes
+    used = [0]
+
+    def remote(src, dst, moves):
+        n = used[0]
+        used[0] += 1
+        return pltpu.make_async_remote_copy(
+            src_ref=src, dst_ref=dst, send_sem=send_sem.at[n], recv_sem=recv_sem.at[n],
+            device_id=peer(moves), device_id_type=pl.DeviceIdType.MESH,
+        )
+
+    def launch(copies):
+        for item in copies:
+            item.start()
+        return copies
+
+    def settle(copies):
+        for item in copies:
+            item.wait()
+
+    core = digit(core_dim)
+    coords = [digit(dim) for dim in slab_dims]
+    mine = [tuple(coords[i] for i in order) for order in slab_orders]
+    dims = [tuple(slab_dims[i] for i in order) for order in slab_orders]
+
     here = {axis: lax.axis_index(axis) for axis in ("scan", "tile")}
     sizes = {axis: lax.axis_size(axis) for axis in ("scan", "tile")}
-
-    def digit(axis, bit):
-        return (here[axis] // bit) % 2
-
-    def partner(axis, bit):
-        return {axis: here[axis] + bit * (1 - 2 * digit(axis, bit))}
-
-    def copy(src, dst, g, step, axis, bit):
-        return pltpu.make_async_remote_copy(
-            src_ref=src, dst_ref=dst, send_sem=send_sem.at[g, step], recv_sem=recv_sem.at[g, step],
-            device_id=partner(axis, bit), device_id_type=pl.DeviceIdType.MESH,
-        )
-
-    plans = []
-    for g in range(pieces):
-        order = [fast_bits[(g + i) % pieces] for i in range(pieces)] + bits[pieces:]
-        steps = []
-        start, size, land = g * piece, piece, 0
-        for axis, bit in order[:halvings]:
-            size //= 2
-            mine = digit(axis, bit)
-            keep, give = start + mine * size, start + (1 - mine) * size
-            steps.append(("halve", axis, bit, give, keep, size, land))
-            start = keep
-            land += size
-        for axis, bit in order[halvings:]:
-            steps.append(("both", axis, bit, start, start, size, land))
-            land += size
-        for axis, bit in reversed(order[:halvings]):
-            low = start - digit(axis, bit) * size
-            steps.append(("gather", axis, bit, start, low + (1 - digit(axis, bit)) * size, size, land))
-            start = low
-            land += size
-            size *= 2
-        plans.append(steps)
-    total = len(plans[0])
-
-    def make(g, step):
-        kind, axis, bit, give, keep, size, land = plans[g][step]
-        source = packed if step == 0 else acc
-        src = source.at[pl.ds(give, size)]
-        return copy(src, landing.at[g, pl.ds(land, size)], g, step, axis, bit)
-
-    def settle(g, step):
-        kind, axis, bit, give, keep, size, land = plans[g][step]
-        source = packed if step == 0 else acc
-        arrived = landing[g, pl.ds(land, size)]
-        acc[pl.ds(keep, size)] = arrived if kind == "gather" else source[pl.ds(keep, size)] + arrived
+    block_rows, block_cols = interior.shape[1:]
 
     def span(shift, block):
         low = {-1: 0, 0: det, 1: det + block}[shift]
@@ -362,21 +365,166 @@
             def _():
                 fold(index).start()
 
+    swap = [launch([remote(packed[q].at[1 - core], land0[q], [(core_dim, 1)])]) for q in range(groups)]
+    swap.append(launch([remote(totals, total_land, [(core_dim, 1)])]))
     interior[...] = frame[:, det : det + block_rows, det : det + block_cols]
-    for g in range(pieces):
-        make(g, 0).start()
+
+    def reduce_start(q, step):
+        dim = dims[q][step]
+        copies = []
+        for d in range(1, dim[2]):
+            spot = mine[q][:step] + (flipped(mine[q][step], dim[2], d),)
+            copies.append(remote(acc[q].at[spot], land[step][q].at[d - 1], [(dim, d)]))
+        return launch(copies)
+
+    def reduce_end(q, step, copies):
+        settle(copies)
+        spot = mine[q][: step + 1]
+        value = acc[q][spot]
+        for d in range(1, dims[q][step][2]):
+            value = value + land[step][q][d - 1]
+        acc[q][spot] = value
+
+    flying = []
+    for q in range(groups):
+        settle(swap[q])
+        acc[q][...] = packed[q][core] + land0[q][...]
+        flying.append(reduce_start(q, 0))
     fold_start((0, 1))
-    for step in range(total):
-        for g in range(pieces):
-            make(g, step).wait()
-            settle(g, step)
-            if step + 1 < total:
-                make(g, step + 1).start()
+    for step in range(3):
+        for q in range(groups):
+            reduce_end(q, step, flying[q])
+            if step < 2:
+                flying[q] = reduce_start(q, step + 1)
         if step == 0:
             fold_start((2, 3))
         if step == 1:
             fold_start((4, 5, 6, 7))
-    out[...] = acc[...]
+    for e, dim in enumerate(extra):
+        for q in range(groups):
+            flying[q] = launch([remote(acc[q].at[mine[q]], landx[q].at[e], [(dim, 1)])])
+        for q in range(groups):
+            settle(flying[q])
+            acc[q][mine[q]] = acc[q][mine[q]] + landx[q][e]
+
+    tile = coords[0]
+    for i in range(1, 3):
+        tile = tile * slab_dims[i][2] + coords[i]
+    strip = pl.ds(pl.multiple_of(tile * rows, rows), rows)
+    scale = 1.0 / (acc[groups - 1][mine[groups - 1] + (per,)] + probe_reg)
+    own = []
+    for q in range(groups):
+        for i in range(per):
+            k, c = plane_of(core, q, i, modes)
+            full[q][(core,) + mine[q] + (i,)] = probe[k, c, strip, :] + acc[q][mine[q] + (i,)] * scale
+        spot = (core,) + mine[q]
+        own.append(remote(full[q].at[spot], full[q].at[spot], [(core_dim, 1)]))
+        launch([own[q]])
+
+    def gather_start(q, step):
+        dim = dims[q][step]
+        spot = (core,) + mine[q][: step + 1]
+        return launch([remote(full[q].at[spot], full[q].at[spot], [(dim, d)]) for d in range(1, dim[2])])
+
+    def pass_on(q, step):
+        dim = dims[q][step]
+        copies = []
+        for d in range(1, dim[2]):
+            spot = (core,) + mine[q][:step] + (flipped(mine[q][step], dim[2], d),)
+            copies.append(remote(full[q].at[spot], full[q].at[spot], [(core_dim, 1)]))
+        return launch(copies)
+
+    flying = [gather_start(q, 2) for q in range(groups)]
+    handed = []
+
+    def slab_rows(spots):
+        values = []
+        for p in range(planes):
+            c, k = p // modes, p % modes
+            half, rest = k // (modes // 2), k % (modes // 2)
+            q, m = rest // (per // 2), rest % (per // 2)
+            values.append(full[q][(half,) + spots[q] + (2 * m + c,)])
+        return jnp.concatenate(values, axis=0)
+
+    tall = planes * rows
+    up = lax.broadcasted_iota(jnp.int32, (tall, tall), 0)
+    across = lax.broadcasted_iota(jnp.int32, (tall, tall), 1)
+    same = jnp.where(((up - across) & (rows - 1)) == 0, 1.0, 0.0).astype(f32)
+    plane = lax.broadcasted_iota(jnp.int32, (planes, tall), 0) * rows
+    entry = lax.broadcasted_iota(jnp.int32, (planes, tall), 1)
+    pick = jnp.where((entry >= plane) & (entry < plane + rows), 1.0, 0.0).astype(f32)
+    plane = lax.broadcasted_iota(jnp.int32, (tall, det), 1) * rows
+    entry = lax.broadcasted_iota(jnp.int32, (tall, det), 0)
+    place = jnp.where((entry >= plane) & (entry < plane + rows), 1.0, 0.0).astype(f32)
+
+    settle(own)
+    held = slab_rows(mine)
+    turned = jnp.concatenate([-held[tall // 2 :], held[: tall // 2]], axis=0)
+    wide = jnp.concatenate([held, turned], axis=1)
+    pairs = lax.dot_general(
+        wide, wide, (((1,), (1,)), ((), ())), precision=highest, preferred_element_type=f32
+    )
+    gram = full_dot(full_dot(pick, pairs * same), place)
+    settle(swap[groups])
+    sums = [jnp.sum(totals[i] + total_land[i]) for i in range(2)]
+    lanes = lax.broadcasted_iota(jnp.int32, (8, det), 1)
+    first = lax.broadcasted_iota(jnp.int32, (8, det), 0) == 0
+    sheet = jnp.where(first & (lanes == det - 2), sums[0], jnp.where(first & (lanes == det - 1), sums[1], 0.0))
+    for part in range(planes // 8):
+        piece = gram[part * 8 : (part + 1) * 8]
+        sheet = sheet + (pltpu.roll(piece, part * 32, 1) if part else piece)
+    gram_out[...] = sheet
+    spread = []
+    slot = 0
+    for d0 in range(slab_dims[0][2]):
+        for d1 in range(slab_dims[1][2]):
+            for d2 in range(slab_dims[2][2]):
+                if d0 + d1 + d2:
+                    moves = list(zip(slab_dims, (d0, d1, d2)))
+                    spread.append(remote(gram_out, gram_land.at[slot], moves))
+                    slot += 1
+    launch(spread)
+    for step in (2, 1):
+        for q in range(groups):
+            settle(flying[q])
+            flying[q] = gather_start(q, step - 1)
+            handed += pass_on(q, step)
+    settle(spread)
+    sheet = gram_out[...]
+    for i in range(slab_count - 1):
+        sheet = sheet + gram_land[i]
+    for e, dim in enumerate(extra):
+        gram_x[2 * e] = sheet
+        item = launch([remote(gram_x.at[2 * e], gram_x.at[2 * e + 1], [(dim, 1)])])
+        settle(item)
+        sheet = sheet + gram_x[2 * e + 1]
+    measured = jnp.sum(jnp.where(first & (lanes == det - 2), sheet, 0.0))
+    modelled = jnp.sum(jnp.where(first & (lanes == det - 1), sheet, 0.0))
+    ratio = measured / (modelled + total_eps)
+    parts = [sheet[:, part * 32 : part * 32 + planes] for part in range(planes // 8)]
+    embedded = jnp.concatenate(parts, axis=0)
+    eye = jnp.where(
+        lax.broadcasted_iota(jnp.int32, (planes, planes), 0) == lax.broadcasted_iota(jnp.int32, (planes, planes), 1),
+        1.0, 0.0,
+    ).astype(f32)
+    frobenius = jnp.sqrt(jnp.sum(embedded * embedded, keepdims=True))
+    current = embedded / frobenius
+    inverse = eye
+    for repeat in range(NS_STEPS):
+        factor = 1.5 * eye - 0.5 * full_dot(inverse, current)
+        current = full_dot(current, factor)
+        inverse = full_dot(factor, inverse)
+    weight = jnp.sqrt(ratio * jnp.sum(embedded * eye, axis=1, keepdims=True))
+    mix = weight * (inverse / jnp.sqrt(frobenius))
+    spread_mix = lax.dot_general(
+        pick, full_dot(mix, pick), (((0,), (0,)), ((), ())), precision=highest, preferred_element_type=f32
+    )
+    high, low = halves(spread_mix * same)
+    mixer = jnp.concatenate([high, low, high], axis=1)
+    for q in range(groups):
+        settle(flying[q])
+        handed += pass_on(q, 0)
+
     for index, (shift_rows, shift_cols) in enumerate(directions()):
         @pl.when(valid(shift_rows, shift_cols))
         def _():
@@ -385,46 +533,68 @@
         @pl.when(valid(-shift_rows, -shift_cols))
         def _():
             fold(index).wait_recv()
-            rows, cols = inner(shift_rows, block_rows), inner(shift_cols, block_cols)
-            interior[:, rows, cols] = interior[:, rows, cols] + slots[index][...]
-
-
-def exchange(packed, frame, det, block_rows, block_cols):
+            r, c = inner(shift_rows, block_rows), inner(shift_cols, block_cols)
+            interior[:, r, c] = interior[:, r, c] + slots[index][...]
+    new_specimen[...] = specimen[...] + interior[0:2] / (interior[2] + object_reg)[None]
+
+    settle(handed)
+    for t in range(0, slab_count, 2):
+        sides = []
+        for s in (t, t + 1):
+            at = slab_coords(s)
+            sides.append(slab_rows([tuple(at[i] for i in order) for order in slab_orders]))
+        high, low = halves(jnp.concatenate(sides, axis=1))
+        out = jnp.dot(mixer, jnp.concatenate([high, high, low], axis=0), preferred_element_type=f32)
+        for p in range(planes):
+            for s in range(2):
+                new_probe[p % modes, p // modes, (t + s) * rows : (t + s + 1) * rows, :] = out[
+                    p * rows : (p + 1) * rows, s * det : (s + 1) * det
+                ]
+
+
+def finish(packed, totals, frame, probe_modes, specimen):
     f32 = jnp.float32
-    bits = mesh_bits()
-    pieces = len(fast_bits)
-    piece = packed.shape[0] // pieces
-    steps = len(bits) + halvings
-    small = piece // 2**halvings
-    land = 2 * (piece - small) + (len(bits) - halvings) * small
+    modes, _, det, _ = probe_modes.shape
+    block_rows, block_cols = specimen.shape[1:]
+    extra = extra_bits()
+    shapes = group_shapes(modes, det)
+    planes = 2 * group_modes(modes)
     vmem = pl.BlockSpec(memory_space=pltpu.VMEM)
-    slots = [
-        pltpu.VMEM((3, det if i else block_rows, det if j else block_cols), f32) for i, j in directions()
+    count = max(len(extra), 1)
+    scratch = [pltpu.VMEM(s, f32) for s in shapes] + [pltpu.VMEM(s, f32) for s in shapes]
+    for step in range(3):
+        scratch += [pltpu.VMEM((s[step] - 1,) + s[step + 1 :], f32) for s in shapes]
+    scratch += [pltpu.VMEM((count,) + s[3:], f32) for s in shapes]
+    scratch += [pltpu.VMEM((2,) + s[:3] + (planes,) + s[4:], f32) for s in shapes]
+    scratch += [pltpu.VMEM((3, det if i else block_rows, det if j else block_cols), f32) for i, j in directions()]
+    sems = 80 + 4 * count
+    scratch += [
+        pltpu.VMEM(totals.shape, f32),
+        pltpu.VMEM((8, det), f32),
+        pltpu.VMEM((slab_count - 1, 8, det), f32),
+        pltpu.VMEM((2 * count, 8, det), f32),
+        pltpu.VMEM((3, block_rows, block_cols), f32),
+        pltpu.SemaphoreType.DMA((sems,)),
+        pltpu.SemaphoreType.DMA((sems,)),
+        pltpu.SemaphoreType.DMA((8,)),
+        pltpu.SemaphoreType.DMA((8,)),
     ]
 
     def kernel(*refs):
-        exchange_kernel(bits, *refs)
+        finish_kernel(extra, *refs)
 
     return pl.pallas_call(
         kernel,
-        name="exchange",
+        name="finish",
         out_shape=(
-            jax.ShapeDtypeStruct(packed.shape, f32),
-            jax.ShapeDtypeStruct((3, block_rows, block_cols), f32),
+            jax.ShapeDtypeStruct(probe_modes.shape, f32),
+            jax.ShapeDtypeStruct(specimen.shape, f32),
         ),
-        in_specs=[vmem, vmem],
+        in_specs=[vmem] * 7,
         out_specs=(vmem, vmem),
-        scratch_shapes=[
-            pltpu.VMEM(packed.shape, f32),
-            pltpu.VMEM((pieces, land) + packed.shape[1:], f32),
-            *slots,
-            pltpu.SemaphoreType.DMA((pieces, steps)),
-            pltpu.SemaphoreType.DMA((pieces, steps)),
-            pltpu.SemaphoreType.DMA((8,)),
-            pltpu.SemaphoreType.DMA((8,)),
-        ],
-        compiler_params=pltpu.CompilerParams(has_side_effects=True, vmem_limit_bytes=40 * 1024 * 1024),
-    )(packed, frame)
+        scratch_shapes=scratch,
+        compiler_params=pltpu.CompilerParams(has_side_effects=True, vmem_limit_bytes=48 * 1024 * 1024),
+    )(*packed, totals, frame, probe_modes, specimen)
 
 
 def halo_kernel(specimen, out, *rest):
@@ -502,24 +672,10 @@
     block_rows = specimen.shape[1]
     block_cols = specimen.shape[2]
     extended = with_halo(specimen, detector)
-    packed, frame_sum = scan_positions(
+    *packed, totals, frame_sum = scan_positions(
         offsets, probe_modes, patterns, extended, block_rows, block_cols
     )
-    summed, interior = exchange(packed, frame_sum, detector, block_rows, block_cols)
-    pixels = detector * detector
-    tiles = detector // 8
-    last = 2 * mode_count * tiles
-    grad_total = summed[:last].reshape(2 * mode_count, pixels)
-    light_total = summed[last : last + tiles].reshape(1, pixels)
-    measured_all = jnp.sum(summed[last + tiles])
-    model_all = jnp.sum(summed[last + tiles + 1])
-    power_ratio = measured_all / (model_all + total_eps)
-    new_specimen = specimen + interior[0:2] / (interior[2] + object_reg)[None]
-    probe_rows = jnp.swapaxes(probe_modes, 0, 1).reshape(2 * mode_count, pixels)
-    updated = probe_rows + grad_total / (light_total + probe_reg)
-    gram_re, gram_im = gram_parts(updated)
-    new_probe = orthonormal_rows(updated, gram_re, gram_im, power_ratio).reshape(probe_modes.shape)
-    return (new_probe, new_specimen)
+    return finish(packed, totals, frame_sum, probe_modes, specimen)
 
 
 def solution(mesh):

time: 135 us -> 99.6 us (0.74)
  matrix products: 13.8 us -> 0 us
  Pallas kernels: 97.2 us -> 89.8 us
  local copies, waits for them, and re-layouts: 16.1 us -> 8.81 us
  other arithmetic: 4.39 us -> 0 us
  between operations: 2.94 us -> 0.67 us
    dot_general x31 -> x0, matrix products: 13.8 us -> none  [the longest x1 1.59 us: gram_parts(): jnp.dot(imag_rows, imag_rows.T, precision=highest, preferred_element_type...]
    pallas_call x2, Pallas kernels: 80.6 us -> 73.2 us  [the longest x1 51.3 us: finish(): pl.pallas_call(kernel, name='finish', out_shape=(jax.ShapeDtypeStruct(pro...]
    unnamed x29 -> x21, local copies, waits for them, and re-layouts: 11.4 us -> 8.81 us
    reshape x1 -> x0, local copies, waits for them, and re-layouts: 2.57 us -> none  [body(): grad_total = summed[:last].reshape(2 * mode_count, pixels)]
    add x3 -> x0, other arithmetic: 1.71 us -> none  [the longest x2 0.97 us: body(): updated = probe_rows + grad_total / (light_total + probe_reg)]
    mul x1 -> x0, other arithmetic: 1.37 us -> none  [orthonormal_rows(): return jnp.stack([ortho_re, ortho_im], axis=1) * weight[:, None, None]]
where the time goes in v1:
time: 99.6 us; the launch traced here: 99.3 us
  Pallas kernels  89.8 us (90%)
  local copies, waits for them, and re-layouts  8.81 us (9%)
    pallas_call x1, Pallas kernels, finish(): pl.pallas_call(kernel, name='finish', out_shape=(jax.ShapeDtypeStruct(pro...  51.3 us
    pallas_call x1, Pallas kernels, scan_positions(): pl.pallas_call(kernel, name='scan_positions', out_shape=(*[jax.ShapeDtype...  21.9 us
    pallas_call x1, Pallas kernels, with_halo(): pl.pallas_call(halo_kernel, name='halo', out_shape=jax.ShapeDtypeStruct((...  16.6 us
    unnamed x21, local copies, waits for them, and re-layouts  8.81 us

profile of v1, /device:TPU:0, one launch (start us, length us, event | category | flops | bytes accessed | tf_op | source)
XLA Modules:
  0.0 99.3 jit_solution(15082263677607834442)
XLA Ops:
  0.6 0.0 copy-start.1
  0.6 0.9 copy.10.refs_0_
  1.5 0.0 copy-start.2
  1.5 0.9 copy-done.2
  2.5 0.0 copy-start.8
  2.5 16.6 %halo.1.refs_3_ = f32[2,384,512]{2,1,0:T(8,128)S(1)} custom-call(f32[2,128,256]{2,1,0:T(8,128)S(1)} %copy-done.2), custom_call_target="tpu_custom_call" | custom-call | tf_op jit(solution)/shard_map/halo/pallas_call | solution.py:658
  19.0 0.0 copy-start
  19.1 1.1 %copy-done = f32[2,384,512]{2,1,0:T(8,128)} copy-done((f32[2,384,512]{2,1,0:T(8,128)}, f32[2,384,512]{2,1,0:T(8,128)S(1)}, u32[]{:S(2)}) %copy-start) | copy-done | bytes 1572888
  20.2 0.0 copy-done.1
  20.2 0.0 copy-done.8
  20.2 0.0 copy-start.4
  20.2 1.0 %copy-done.4 = bf16[768,256]{1,0:T(8,128)(2,1)S(1)} copy-done((bf16[768,256]{1,0:T(8,128)(2,1)S(1)}, bf16[768,256]{1,0:T(8,128)(2,1)}, u32[]{:S(2)}) %copy-start.4) | copy-done | bytes 393240
  21.2 0.0 copy-start.5
  21.2 1.0 %copy-done.5 = bf16[256,768]{1,0:T(8,128)(2,1)S(1)} copy-done((bf16[256,768]{1,0:T(8,128)(2,1)S(1)}, bf16[256,768]{1,0:T(8,128)(2,1)}, u32[]{:S(2)}) %copy-start.5) | copy-done | bytes 393240
  22.2 0.0 copy-start.6
  22.2 1.0 %copy-done.6 = bf16[256,768]{1,0:T(8,128)(2,1)S(1)} copy-done((bf16[256,768]{1,0:T(8,128)(2,1)S(1)}, bf16[256,768]{1,0:T(8,128)(2,1)}, u32[]{:S(2)}) %copy-start.6) | copy-done | bytes 393240
  23.2 0.0 copy-start.7
  23.2 1.0 %copy-done.7 = bf16[768,256]{1,0:T(8,128)(2,1)S(1)} copy-done((bf16[768,256]{1,0:T(8,128)(2,1)S(1)}, bf16[768,256]{1,0:T(8,128)(2,1)}, u32[]{:S(2)}) %copy-start.7) | copy-done | bytes 393240
  24.2 0.0 copy-start.3
  24.2 21.9 %scan_positions.1 = (f32[2,2,2,4,4,8,128]{6,5,4,3,2,1,0:T(8,128)S(1)}, f32[2,2,4,2,4,8,128]{6,5,4,3,2,1,0:T(8,128)S(1)}, f32[2,4,2,2,5,8,128]{6,5,4,3,2,1,0:T(8,...) custom-call(s32[4,2]{1,0:T(4,128)S(1)} %copy.10.refs_0_, f32[12,2,128,128]{3,2,1,0:T(8,128)S(1)} %copy-done.1, ...), custom_call_target="tpu_custom_call" | custom-call | tf_op jit(solution)/shard_map/scan_positions/pallas_call | solution.py:177
  46.1 0.0 copy-done.3
  46.1 51.3 %finish.1 = (f32[12,2,128,128]{3,2,1,0:T(8,128)S(1)}, f32[2,128,256]{2,1,0:T(8,128)S(1)}) custom-call(f32[2,2,2,4,4,8,128]{6,5,4,3,2,1,0:T(8,128)S(1)} %get-tuple-element.7.refs_0_, f32[2,2,4,2,4,8,128]{6,5,4,3,2,1,0:T(8,128)S(1)} %get-tuple-element.8.refs_1_, f32[2,4,2,2,5,8,128]{6,5,4,3,2,1,0:T(8,128)S(1)} %get-tuple-element.9.refs_2_, ...), custom_call_target="tpu_custom_call" | custom-call | tf_op jit(solution)/shard_map/finish/pallas_call | solution.py:586
  97.4 1.1 %copy.13 = f32[12,2,128,128]{3,2,1,0:T(8,128)} copy(f32[12,2,128,128]{3,2,1,0:T(8,128)S(1)} %get-tuple-element.14) | data formatting | bytes 3145728
  98.6 0.7 copy.14
Async XLA Ops:
  0.6 19.6 %copy-start.1 = (f32[12,2,128,128]{3,2,1,0:T(8,128)S(1)}, f32[12,2,128,128]{3,2,1,0:T(8,128)}, u32[]{:S(2)}) copy-start(f32[12,2,128,128]{3,2,1,0:T(8,128)} %refs_5_.2) | copy-start | bytes 4718596
  1.5 0.9 copy-start.2
  2.5 17.7 %copy-start.8 = (f32[4,128,128]{2,1,0:T(8,128)S(1)}, f32[4,128,128]{2,1,0:T(8,128)}, u32[]{:S(2)}) copy-start(f32[4,128,128]{2,1,0:T(8,128)} %refs_2_.1) | copy-start | bytes 786436
  19.0 1.1 %copy-start = (f32[2,384,512]{2,1,0:T(8,128)}, f32[2,384,512]{2,1,0:T(8,128)S(1)}, u32[]{:S(2)}) copy-start(f32[2,384,512]{2,1,0:T(8,128)S(1)} %halo.1.refs_3_) | copy-start | bytes 4718596
  20.2 1.0 %copy-start.4 = (bf16[768,256]{1,0:T(8,128)(2,1)S(1)}, bf16[768,256]{1,0:T(8,128)(2,1)}, u32[]{:S(2)}) copy-start(bf16[768,256]{1,0:T(8,128)(2,1)} %constant.11.clone.refs_7_) | copy-start | bytes 1179652
  21.2 1.0 %copy-start.5 = (bf16[256,768]{1,0:T(8,128)(2,1)S(1)}, bf16[256,768]{1,0:T(8,128)(2,1)}, u32[]{:S(2)}) copy-start(bf16[256,768]{1,0:T(8,128)(2,1)} %constant.10.clone.refs_6_) | copy-start | bytes 1179652
  22.2 1.0 %copy-start.6 = (bf16[256,768]{1,0:T(8,128)(2,1)S(1)}, bf16[256,768]{1,0:T(8,128)(2,1)}, u32[]{:S(2)}) copy-start(bf16[256,768]{1,0:T(8,128)(2,1)} %constant.9.clone.refs_5_) | copy-start | bytes 1179652
  23.2 1.0 %copy-start.7 = (bf16[768,256]{1,0:T(8,128)(2,1)S(1)}, bf16[768,256]{1,0:T(8,128)(2,1)}, u32[]{:S(2)}) copy-start(bf16[768,256]{1,0:T(8,128)(2,1)} %constant.8.clone.refs_4_) | copy-start | bytes 1179652
  24.2 21.9 %copy-start.3 = (f32[2,128,256]{2,1,0:T(8,128)S(1)}, f32[2,128,256]{2,1,0:T(8,128)}, u32[]{:S(2)}) copy-start(f32[2,128,256]{2,1,0:T(8,128)} %refs_6_.2) | copy-start | bytes 786436

commit v2 on v1

v2 whole, which is shorter than its diff:
```python
import math

import jax
import jax.numpy as jnp
import numpy as np
from jax import lax
from jax.experimental import pallas as pl
from jax.experimental.pallas import tpu as pltpu
from jax.sharding import PartitionSpec as P

NS_STEPS = 8


highest = lax.Precision.HIGHEST
light_floor = 0.05
object_reg = 0.5
probe_reg = 1.0
total_eps = 1e-06


def dft_tables(detector):
    indices = np.arange(detector, dtype=np.int64)
    angles = -2.0 * np.pi / detector * (indices[:, None] * indices[None, :] % detector)
    table_re = np.cos(angles) / np.sqrt(detector)
    table_im = np.sin(angles) / np.sqrt(detector)
    right = np.block([[table_re, table_im], [-table_im, table_re]]).astype(np.float32)
    left = np.ascontiguousarray(right.T)
    parts = []
    for table in (right, left):
        high = table.astype(jnp.bfloat16)
        low = (table - high.astype(np.float32)).astype(jnp.bfloat16)
        parts.append((high, low))
    (rh, rl), (lh, ll) = parts
    return (
        np.concatenate([rh, rl, rh], axis=0),
        np.concatenate([lh, ll, lh], axis=1),
        np.concatenate([rh, rl, rh], axis=1),
        np.concatenate([lh, ll, lh], axis=0),
    )


def halves(value):
    high = value.astype(jnp.bfloat16)
    low = (value - high.astype(jnp.float32)).astype(jnp.bfloat16)
    return high, low


core_dim = ("scan", 1, 2)
slab_dims = (("scan", 2, 2), ("tile", 1, 2), ("scan", 4, 4))
slab_orders = ((0, 1, 2), (1, 2, 0), (2, 0, 1))
slab_sizes = tuple(size for _, _, size in slab_dims)
slab_count = math.prod(slab_sizes)
groups = len(slab_orders)


def extra_bits():
    bits = []
    for axis, bit in (("scan", 16), ("tile", 2)):
        while bit < lax.axis_size(axis):
            bits.append((axis, bit, 2))
            bit *= 2
    return bits


def group_planes(modes, q):
    return modes // groups + (q == 0)


def slab_coords(tile):
    coords = []
    for size in reversed(slab_sizes):
        coords.append(tile % size)
        tile = tile // size
    return tuple(coords[::-1])


def directions():
    return [(i, j) for i, j in ((1, 0), (-1, 0), (0, 1), (0, -1), (1, 1), (1, -1), (-1, 1), (-1, -1))]


def digit(dim):
    axis, bit, size = dim
    return (lax.axis_index(axis) // bit) % size


def flipped(value, size, d):
    if size == 2:
        return 1 - value if d else value
    low, high = value % 2, value // 2
    low = 1 - low if d % 2 else low
    high = 1 - high if d // 2 else high
    return low + 2 * high


def peer(moves):
    where = {}
    for dim, d in moves:
        axis, bit, size = dim
        here = digit(dim)
        base = where.get(axis, lax.axis_index(axis))
        where[axis] = base + bit * (flipped(here, size, d) - here)
    return where


def full_dot(a, b):
    return jnp.dot(a, b, precision=highest, preferred_element_type=jnp.float32)


def zeros_into(ref):
    ref[...] = jnp.zeros(ref.shape, ref.dtype)


def update_kernel(extra, names, *refs):
    f32 = jnp.float32
    r = dict(zip(names, refs))
    offs, probe_in, patterns_in, specimen_in = r["offs"], r["probe_in"], r["patterns_in"], r["specimen_in"]
    new_probe, new_specimen = r["new_probe"], r["new_specimen"]
    probe, patterns, specimen, tables = r["probe"], r["patterns"], r["specimen"], [r[f"table{n}"] for n in range(4)]
    ext, pads, frame_num, frame_light = r["ext"], r["pads"], r["frame_num"], r["frame_light"]
    deep, half, far, patch, factor, num = r["deep"], r["half"], r["far"], r["patch"], r["factor"], r["num"]
    power, light, totals, total_land = r["power"], r["light"], r["totals"], r["total_land"]
    packed = [r[f"packed{q}"] for q in range(groups)]
    land0 = [r[f"land0_{q}"] for q in range(groups)]
    acc = [r[f"acc{q}"] for q in range(groups)]
    land = [[r[f"land{s}_{q}"] for q in range(groups)] for s in (1, 2, 3)]
    landx = [r[f"landx{q}"] for q in range(groups)]
    full = [r[f"full{q}"] for q in range(groups)]
    num_slots = [r[f"num_slot{i}"] for i in range(8)]
    light_slots = [r[f"light_slot{i}"] for i in range(8)]
    gram_out, gram_land, gram_x, interior = r["gram_out"], r["gram_land"], r["gram_x"], r["interior"]
    send_sem, recv_sem, local_sem = r["send_sem"], r["recv_sem"], r["local_sem"]
    right_f, left_f, left_b, right_b = tables

    modes, det = probe.shape[0], probe.shape[-1]
    count = patterns.shape[0]
    block_rows, block_cols = specimen.shape[1:]
    own_blocks = block_cols // det
    col_blocks = own_blocks + 2
    ext_rows = block_rows + 2 * det
    per = modes // groups
    pair = per // 2
    rows = det // slab_count
    planes = 2 * modes
    used = [0]

    here = {axis: lax.axis_index(axis) for axis in ("scan", "tile")}
    sizes = {axis: lax.axis_size(axis) for axis in ("scan", "tile")}

    def route(src, dst, device):
        n = used[0]
        used[0] += 1
        return pltpu.make_async_remote_copy(
            src_ref=src, dst_ref=dst, send_sem=send_sem.at[n], recv_sem=recv_sem.at[n],
            device_id=device, device_id_type=pl.DeviceIdType.MESH,
        )

    def remote(src, dst, moves):
        return route(src, dst, peer(moves))

    def shifted(i, j):
        return {
            "scan": (here["scan"] + i + sizes["scan"]) % sizes["scan"],
            "tile": (here["tile"] + j + sizes["tile"]) % sizes["tile"],
        }

    def valid(i, j):
        row, col = here["scan"] + i, here["tile"] + j
        return (row >= 0) & (row < sizes["scan"]) & (col >= 0) & (col < sizes["tile"])

    def launch(copies):
        for item in copies:
            item.start()
        return copies

    def settle(copies):
        for item in copies:
            item.wait()

    core = digit(core_dim)
    mine = [digit(dim) for dim in slab_dims]

    off_shift, on_shift = 2 * core - 1, 1 - 2 * core

    def outer_rows(i):
        return pl.ds(pl.multiple_of((1 - i) // 2 * (det + block_rows), 8), det)

    def edge_rows(i, base):
        return pl.ds(pl.multiple_of(base + (1 + i) // 2 * (block_rows - det), 8), det)

    def edge_block(j):
        return own_blocks - 1 if j == 1 else 0

    def outer_block(j):
        return 0 if j == 1 else own_blocks + 1

    off_valid = valid(off_shift, 0)
    edges = sorted({0, own_blocks - 1})
    inner_blocks = [b for b in range(own_blocks) if b not in edges]
    local = []

    def load(src, dst):
        item = pltpu.make_async_copy(src, dst, local_sem.at[len(local)])
        item.start()
        local.append(item)
        return item

    def row_copies(i, blocks):
        copies = []
        for b in blocks:
            copies.append(
                route(
                    specimen_in.at[:, edge_rows(i, 0), b * det : (b + 1) * det],
                    ext.at[:, 1 + b, outer_rows(i), :],
                    shifted(i, 0),
                )
            )
        return copies

    off_rows = row_copies(off_shift, edges + inner_blocks)
    on_rows = row_copies(on_shift, edges + inner_blocks)

    @pl.when(off_valid)
    def _():
        launch(off_rows[: len(edges)])

    side = {}
    for j in (1, -1):
        b = edge_block(j)
        side[j] = route(
            specimen_in.at[:, :, b * det : (b + 1) * det],
            ext.at[:, outer_block(j), pl.ds(det, block_rows), :],
            shifted(0, j),
        )

        @pl.when(valid(0, j))
        def _():
            side[j].start()

    launch(on_rows)
    if inner_blocks:
        @pl.when(off_valid)
        def _():
            launch(off_rows[len(edges) :])

    probe_load = load(probe_in, probe)
    own_load = [
        load(specimen_in.at[:, :, b * det : (b + 1) * det], ext.at[:, 1 + b, pl.ds(det, block_rows), :])
        for b in range(own_blocks)
    ]
    other_loads = [load(patterns_in, patterns), load(specimen_in, specimen)]
    for n in range(4):
        other_loads.append(load(r[f"table_in{n}"], tables[n]))

    blank = jnp.zeros((2, det, det), f32)
    zeros_into(ext.at[:, col_blocks])

    @pl.when(jnp.logical_not(off_valid))
    def _():
        for b in range(col_blocks):
            ext[:, b, outer_rows(-off_shift), :] = blank

    for j in (1, -1):
        @pl.when(jnp.logical_not(valid(0, -j)))
        def _():
            ext[:, outer_block(j), pl.ds(det, block_rows), :] = jnp.zeros((2, block_rows, det), f32)
            ext[:, outer_block(j), outer_rows(1), :] = blank
            ext[:, outer_block(j), outer_rows(-1), :] = blank

    zeros_into(pads)
    for q in range(groups):
        zeros_into(packed[q])
    zeros_into(light)

    lanes = lax.broadcasted_iota(jnp.int32, (det, det), 1)
    row_base = here["scan"] * block_rows - det
    col_base = here["tile"] * block_cols - det

    def place(p):
        row = jnp.clip(offs[p, 0] - row_base, 0, block_rows + det)
        col = jnp.clip(offs[p, 1] - col_base, 0, block_cols + det)
        block = col // det
        return row, col, block, col - block * det

    def build_frame(frame, channels):
        chunk = 64
        strip_lanes = lax.broadcasted_iota(jnp.int32, (chunk, det), 1)

        def some(n, carry):
            base = pl.multiple_of(n * chunk, chunk)
            for c in range(channels):
                values = [jnp.zeros((chunk, det), f32) for _ in range(col_blocks)]
                for p in range(count):
                    row, col, _, _ = place(p)
                    piece = pads[p, c, pl.ds(ext_rows - det - row + base, chunk), :]
                    for j in range(col_blocks):
                        at = strip_lanes + (j * det - col)
                        values[j] = values[j] + jnp.where((at >= 0) & (at < det), piece, 0.0)
                for j in range(col_blocks):
                    frame[c, pl.ds(base, chunk), j * det : (j + 1) * det] = values[j]
            return carry

        lax.fori_loop(0, ext_rows // chunk, some, 0)

    pad_at = pl.ds(ext_rows - det, det)
    probe_load.wait()
    value = jnp.zeros((det, det), f32)
    for k in range(modes):
        value = value + probe[k, 0] * probe[k, 0] + probe[k, 1] * probe[k, 1]
    power[...] = value
    for p in range(count):
        pads[p, 0, pad_at, :] = pltpu.roll(power[...], place(p)[3], 1)
    build_frame(frame_light, 1)

    @pl.when(off_valid)
    def _():
        for item in off_rows[: len(edges)]:
            item.wait()

    relay = []
    for j in (1, -1):
        b = edge_block(j)
        item = route(
            ext.at[:, 1 + b, outer_rows(-off_shift), :],
            ext.at[:, outer_block(j), outer_rows(-off_shift), :],
            shifted(0, j),
        )
        relay.append((item, off_valid & valid(0, j), off_valid & valid(0, -j)))

        @pl.when(off_valid & valid(0, j))
        def _():
            item.start()

    for j in (1, -1):
        @pl.when(valid(0, j))
        def _():
            side[j].wait_send()

        item = route(
            ext.at[:, outer_block(j), edge_rows(on_shift, det), :],
            ext.at[:, outer_block(j), outer_rows(on_shift), :],
            shifted(on_shift, 0),
        )
        relay.append((item, valid(0, -j), valid(0, -j)))

        @pl.when(valid(0, -j))
        def _():
            side[j].wait_recv()
            item.start()

    settle(on_rows)
    if inner_blocks:
        @pl.when(off_valid)
        def _():
            settle(off_rows[len(edges) :])
    for item, sent, came in relay:
        @pl.when(sent)
        def _():
            item.wait_send()

        @pl.when(came)
        def _():
            item.wait_recv()
    for item in own_load + other_loads:
        item.wait()

    def span(shift, block):
        low = {-1: 0, 0: det, 1: det + block}[shift]
        return pl.ds(low, block if shift == 0 else det)

    def inner(shift, block):
        low = {-1: block - det, 0: 0, 1: 0}[shift]
        return pl.ds(low, block if shift == 0 else det)

    def fold_copies(frame, slots):
        copies = []
        for index, (i, j) in enumerate(directions()):
            copies.append(
                route(frame.at[:, span(i, block_rows), span(j, block_cols)], slots[index], shifted(i, j))
            )
        return copies

    def fold_start(copies, indices):
        for index in indices:
            @pl.when(valid(*directions()[index]))
            def _():
                copies[index].start()

    def fold_end(copies, slots, into):
        for index, (i, j) in enumerate(directions()):
            @pl.when(valid(i, j))
            def _():
                copies[index].wait_send()

            @pl.when(valid(-i, -j))
            def _():
                copies[index].wait_recv()
                a, b = inner(i, block_rows), inner(j, block_cols)
                interior[into, a, b] = interior[into, a, b] + slots[index][...]

    light_fold = fold_copies(frame_light, light_slots)
    fold_start(light_fold, range(8))

    def forward(p, total):
        row, _, block, shift = place(p)
        back = lax.rem(det - shift, det)

        def patch_part(c):
            first = pltpu.roll(ext[c, block, pl.ds(row, det), :], back, 1)
            second = pltpu.roll(ext[c, block + 1, pl.ds(row, det), :], back, 1)
            return jnp.where(lanes < det - shift, first, second)

        patch_re = patch_part(0)
        patch_im = patch_part(1)
        patch[p, 0] = patch_re
        patch[p, 1] = patch_im
        patch_light = patch_re * patch_re + patch_im * patch_im
        light[...] = light[...] + patch_light
        total = total + patch_light * power[...]
        for k in range(modes):
            at = pl.ds(k * det, det)
            pr, pi = probe[k, 0], probe[k, 1]
            for c, value in enumerate((pr * patch_re - pi * patch_im, pr * patch_im + pi * patch_re)):
                high, low = halves(value)
                deep[at, pl.ds(c * det, det)] = high
                deep[at, pl.ds((2 + c) * det, det)] = high
                deep[at, pl.ds((4 + c) * det, det)] = low
        half[...] = jnp.dot(deep[...], right_f[...], preferred_element_type=f32)
        model = jnp.zeros((det, det), f32)
        for k in range(0, modes, 2):
            lo_at, hi_at = pl.ds(k * det, det), pl.ds((k + 1) * det, det)
            first, second = half[lo_at, :], half[hi_at, :]
            paired = jnp.concatenate(
                [
                    jnp.concatenate([first[:, :det], second[:, :det]], axis=1),
                    jnp.concatenate([first[:, det:], second[:, det:]], axis=1),
                ],
                axis=0,
            )
            high, low = halves(paired)
            stacked = jnp.concatenate([high, high, low], axis=0)
            out = jnp.dot(left_f[...], stacked, preferred_element_type=f32)
            far[p, :, pl.ds(k * det, 2 * det)] = out
            squares = out * out
            both = squares[:det] + squares[det:]
            model = model + both[:, :det] + both[:, det:]
        factor[p] = jnp.sqrt(patterns[p]) / jnp.sqrt(jnp.maximum(model, light_floor)) - 1.0
        return total

    total = lax.fori_loop(0, count, forward, jnp.zeros((det, det), f32))
    measured = jnp.zeros((det, det), f32)
    for p in range(count):
        measured = measured + patterns[p]
    totals[0] = jnp.sum(measured.reshape(det // 8, 8, det), axis=0)
    totals[1] = jnp.sum(total.reshape(det // 8, 8, det), axis=0)
    spread_shape = slab_sizes + (rows, det)
    for h in range(2):
        packed[0][h, :, :, :, per] = light[...].reshape(spread_shape)

    def spot_of(q, known, last=None):
        spot = [slice(None)] * 3
        for n in range(known):
            spot[slab_orders[q][n]] = mine[slab_orders[q][n]]
        if last is not None:
            spot[slab_orders[q][known]] = last
        return tuple(spot)

    def other(q, step, d):
        i = slab_orders[q][step]
        return flipped(mine[i], slab_sizes[i], d)

    def reach(q, step):
        return slab_dims[slab_orders[q][step]]

    swap = [remote(packed[q].at[1 - core], land0[q], [(core_dim, 1)]) for q in range(groups)]
    total_swap = remote(totals, total_land, [(core_dim, 1)])
    reducing = []
    for q in range(groups):
        reducing.append([])
        for step in range(3):
            dim = reach(q, step)
            reducing[q].append(
                [
                    remote(acc[q].at[spot_of(q, step, other(q, step, d))], land[step][q].at[d - 1], [(dim, d)])
                    for d in range(1, dim[2])
                ]
            )

    def swap_end(q):
        swap[q].wait()
        acc[q][...] = packed[q][core] + land0[q][...]
        launch(reducing[q][0])

    def reduce_end(q, step):
        settle(reducing[q][step])
        spot = spot_of(q, step + 1)
        value = acc[q][spot]
        for d in range(1, reach(q, step)[2]):
            value = value + land[step][q][d - 1]
        acc[q][spot] = value
        if step < 2:
            launch(reducing[q][step + 1])

    def backward(q, events):
        def one(p, carry):
            for when, event in events:
                @pl.when(p == when)
                def _():
                    event()

            wide = jnp.concatenate([factor[p], factor[p]], axis=1)
            wide = jnp.concatenate([wide, wide], axis=0)
            chosen = [h * (modes // 2) + q * pair + m for h in range(2) for m in range(pair)]
            for n in range(0, per, 2):
                high, low = halves(far[p, :, pl.ds(chosen[n] * det, 2 * det)] * wide)
                stacked = jnp.concatenate([high, high, low], axis=0)
                out = jnp.dot(left_b[...], stacked, preferred_element_type=f32)
                high, low = halves(out)
                for m in range(2):
                    at = pl.ds((n + m) * det, det)
                    for c in range(2):
                        part_h = high[c * det : (c + 1) * det, m * det : (m + 1) * det]
                        part_l = low[c * det : (c + 1) * det, m * det : (m + 1) * det]
                        deep[at, pl.ds(c * det, det)] = part_h
                        deep[at, pl.ds((2 + c) * det, det)] = part_h
                        deep[at, pl.ds((4 + c) * det, det)] = part_l
            some = pl.ds(0, per * det)
            half[some, :] = jnp.dot(deep[some, :], right_b[...], preferred_element_type=f32)
            patch_re, patch_im = patch[p, 0], patch[p, 1]
            num_re = jnp.zeros((det, det), f32)
            num_im = jnp.zeros((det, det), f32)
            for n, k in enumerate(chosen):
                at = pl.ds(n * det, det)
                cr, ci = half[at, :det], half[at, det:]
                pr, pi = probe[k, 0], probe[k, 1]
                h, i = n // pair, n % pair
                for c, value in enumerate((patch_re * cr + patch_im * ci, patch_re * ci - patch_im * cr)):
                    spot = (h, slice(None), slice(None), slice(None), 2 * i + c)
                    packed[q][spot] = packed[q][spot] + value.reshape(spread_shape)
                num_re = num_re + pr * cr + pi * ci
                num_im = num_im + pr * ci - pi * cr
            if q:
                num_re = num_re + num[p, 0]
                num_im = num_im + num[p, 1]
            if q < groups - 1:
                num[p, 0] = num_re
                num[p, 1] = num_im
            else:
                shift = place(p)[3]
                pads[p, 0, pad_at, :] = pltpu.roll(num_re, shift, 1)
                pads[p, 1, pad_at, :] = pltpu.roll(num_im, shift, 1)
            return carry

        lax.fori_loop(0, count, one, 0)

    backward(0, [])
    swap[0].start()
    total_swap.start()
    backward(1, [(2, lambda: swap_end(0))])
    swap[1].start()
    backward(2, [(2, lambda: (swap_end(1), reduce_end(0, 0)))])
    swap[2].start()
    build_frame(frame_num, 2)
    num_fold = fold_copies(frame_num, num_slots)
    reduce_end(0, 1)
    swap_end(2)
    fold_start(num_fold, (0, 1))
    reduce_end(1, 0)
    reduce_end(0, 2)
    fold_start(num_fold, (2, 3))
    reduce_end(1, 1)
    reduce_end(2, 0)
    fold_start(num_fold, (4, 5, 6, 7))

    tile = mine[0]
    for i in range(1, 3):
        tile = tile * slab_sizes[i] + mine[i]
    strip = pl.ds(pl.multiple_of(tile * rows, rows), rows)
    home = tuple(mine)
    own = [remote(full[q].at[(core,) + home], full[q].at[(core,) + home], [(core_dim, 1)]) for q in range(groups)]
    gathering, passing = [], []
    for q in range(groups):
        gathering.append([])
        passing.append([])
        for step in range(3):
            dim = reach(q, step)
            spot = (core,) + spot_of(q, step + 1)
            gathering[q].append(
                [remote(full[q].at[spot], full[q].at[spot], [(dim, d)]) for d in range(1, dim[2])]
            )
            passed = []
            for d in range(1, dim[2]):
                spot = (core,) + spot_of(q, step, other(q, step, d))
                passed.append(remote(full[q].at[spot], full[q].at[spot], [(core_dim, 1)]))
            passing[q].append(passed)

    def update_slab(q):
        for e, dim in enumerate(extra):
            item = remote(acc[q].at[home], landx[q].at[e], [(dim, 1)])
            item.start()
            item.wait()
            acc[q][home] = acc[q][home] + landx[q][e]
        scale = 1.0 / (acc[0][home + (per,)] + probe_reg)
        for i in range(per):
            k = core * (modes // 2) + q * pair + i // 2
            full[q][(core,) + home + (i,)] = probe[k, i % 2, strip, :] + acc[q][home + (i,)] * scale
        own[q].start()
        launch(gathering[q][2])

    def gather_end(q, step):
        settle(gathering[q][step])
        if step:
            launch(gathering[q][step - 1])
        launch(passing[q][step])

    update_slab(0)
    reduce_end(1, 2)
    update_slab(1)
    reduce_end(2, 1)
    gather_end(0, 2)
    reduce_end(2, 2)
    update_slab(2)
    gather_end(1, 2)
    gather_end(0, 1)

    def slab_rows(spot):
        values = []
        for n in range(planes):
            c, k = n // modes, n % modes
            h, rest = k // (modes // 2), k % (modes // 2)
            q, m = rest // pair, rest % pair
            values.append(full[q][(h,) + spot + (2 * m + c,)])
        return jnp.concatenate(values, axis=0)

    tall = planes * rows
    up = lax.broadcasted_iota(jnp.int32, (tall, tall), 0)
    across = lax.broadcasted_iota(jnp.int32, (tall, tall), 1)
    same = jnp.where(((up - across) & (rows - 1)) == 0, 1.0, 0.0).astype(f32)
    plane = lax.broadcasted_iota(jnp.int32, (planes, tall), 0) * rows
    entry = lax.broadcasted_iota(jnp.int32, (planes, tall), 1)
    pick = jnp.where((entry >= plane) & (entry < plane + rows), 1.0, 0.0).astype(f32)
    plane = lax.broadcasted_iota(jnp.int32, (tall, det), 1) * rows
    entry = lax.broadcasted_iota(jnp.int32, (tall, det), 0)
    settled = jnp.where((entry >= plane) & (entry < plane + rows), 1.0, 0.0).astype(f32)

    settle(own)
    held = slab_rows(home)
    turned = jnp.concatenate([-held[tall // 2 :], held[: tall // 2]], axis=0)
    wide = jnp.concatenate([held, turned], axis=1)
    pairs = lax.dot_general(
        wide, wide, (((1,), (1,)), ((), ())), precision=highest, preferred_element_type=f32
    )
    gram = full_dot(full_dot(pick, pairs * same), settled)
    total_swap.wait()
    sums = [jnp.sum(totals[i] + total_land[i]) for i in range(2)]
    sheet_lanes = lax.broadcasted_iota(jnp.int32, (8, det), 1)
    first = lax.broadcasted_iota(jnp.int32, (8, det), 0) == 0
    at_measured = first & (sheet_lanes == det - 2)
    at_modelled = first & (sheet_lanes == det - 1)
    sheet = jnp.where(at_measured, sums[0], jnp.where(at_modelled, sums[1], 0.0))
    for part in range(planes // 8):
        piece = gram[part * 8 : (part + 1) * 8]
        sheet = sheet + (pltpu.roll(piece, part * 32, 1) if part else piece)
    gram_out[...] = sheet
    spread = []
    for slot in range(1, slab_count):
        moves = list(zip(slab_dims, slab_coords(slot)))
        spread.append(remote(gram_out, gram_land.at[slot - 1], moves))
    launch(spread)
    gather_end(2, 2)
    gather_end(1, 1)
    gather_end(2, 1)
    settle(spread)
    sheet = gram_out[...]
    for i in range(slab_count - 1):
        sheet = sheet + gram_land[i]
    for e, dim in enumerate(extra):
        gram_x[2 * e] = sheet
        item = remote(gram_x.at[2 * e], gram_x.at[2 * e + 1], [(dim, 1)])
        item.start()
        item.wait()
        sheet = sheet + gram_x[2 * e + 1]
    measured = jnp.sum(jnp.where(at_measured, sheet, 0.0))
    modelled = jnp.sum(jnp.where(at_modelled, sheet, 0.0))
    ratio = measured / (modelled + total_eps)
    parts = [sheet[:, part * 32 : part * 32 + planes] for part in range(planes // 8)]
    embedded = jnp.concatenate(parts, axis=0)
    eye = jnp.where(
        lax.broadcasted_iota(jnp.int32, (planes, planes), 0) == lax.broadcasted_iota(jnp.int32, (planes, planes), 1),
        1.0, 0.0,
    ).astype(f32)
    frobenius = jnp.sqrt(jnp.sum(embedded * embedded, keepdims=True))
    current = embedded / frobenius
    inverse = eye
    for repeat in range(NS_STEPS):
        scaled = 1.5 * eye - 0.5 * full_dot(inverse, current)
        current = full_dot(current, scaled)
        inverse = full_dot(scaled, inverse)
    weight = jnp.sqrt(ratio * jnp.sum(embedded * eye, axis=1, keepdims=True))
    mix = weight * (inverse / jnp.sqrt(frobenius))
    mix = lax.dot_general(
        pick, full_dot(mix, pick), (((0,), (0,)), ((), ())), precision=highest, preferred_element_type=f32
    )
    high, low = halves(mix * same)
    mixer = jnp.concatenate([high, low, high], axis=1)
    for q in range(groups):
        gather_end(q, 0)

    interior[0:2] = frame_num[:, det : det + block_rows, det : det + block_cols]
    interior[2] = frame_light[0, det : det + block_rows, det : det + block_cols]
    fold_end(light_fold, light_slots, slice(2, 3))
    fold_end(num_fold, num_slots, slice(0, 2))
    new_specimen[...] = specimen[...] + interior[0:2] / (interior[2] + object_reg)[None]

    for q in range(groups):
        for step in range(3):
            settle(passing[q][step])
    for t in range(0, slab_count, 2):
        sides = [slab_rows(slab_coords(s)) for s in (t, t + 1)]
        high, low = halves(jnp.concatenate(sides, axis=1))
        out = jnp.dot(mixer, jnp.concatenate([high, high, low], axis=0), preferred_element_type=f32)
        for n in range(planes):
            for s in range(2):
                new_probe[n % modes, n // modes, (t + s) * rows : (t + s + 1) * rows, :] = out[
                    n * rows : (n + 1) * rows, s * det : (s + 1) * det
                ]


def body(probe_modes, patterns, specimen, offsets):
    f32 = jnp.float32
    modes, _, det, _ = probe_modes.shape
    count = patterns.shape[0]
    block_rows, block_cols = specimen.shape[1:]
    col_blocks = block_cols // det + 2
    ext_rows = block_rows + 2 * det
    ext_cols = block_cols + 2 * det
    extra = extra_bits()
    more = max(len(extra), 1)
    rows = det // slab_count
    bf16 = jnp.bfloat16
    tables = [jnp.asarray(t) for t in dft_tables(det)]
    sems = 160 + 6 * more
    scratch = {
        "probe": pltpu.VMEM(probe_modes.shape, f32),
        "patterns": pltpu.VMEM(patterns.shape, f32),
        "specimen": pltpu.VMEM(specimen.shape, f32),
        **{f"table{n}": pltpu.VMEM(t.shape, bf16) for n, t in enumerate(tables)},
        "ext": pltpu.VMEM((2, col_blocks + 1, ext_rows, det), f32),
        "pads": pltpu.VMEM((count, 2, 2 * (ext_rows - det) + det, det), f32),
        "frame_num": pltpu.VMEM((2, ext_rows, ext_cols), f32),
        "frame_light": pltpu.VMEM((1, ext_rows, ext_cols), f32),
        "deep": pltpu.VMEM((modes * det, 6 * det), bf16),
        "half": pltpu.VMEM((modes * det, 2 * det), f32),
        "far": pltpu.VMEM((count, 2 * det, modes * det), f32),
        "patch": pltpu.VMEM((count, 2, det, det), f32),
        "factor": pltpu.VMEM((count, det, det), f32),
        "num": pltpu.VMEM((count, 2, det, det), f32),
        "power": pltpu.VMEM((det, det), f32),
        "light": pltpu.VMEM((det, det), f32),
        "totals": pltpu.VMEM((2, 8, det), f32),
        "total_land": pltpu.VMEM((2, 8, det), f32),
        "gram_out": pltpu.VMEM((8, det), f32),
        "gram_land": pltpu.VMEM((slab_count - 1, 8, det), f32),
        "gram_x": pltpu.VMEM((2 * more, 8, det), f32),
        "interior": pltpu.VMEM((3, block_rows, block_cols), f32),
        "send_sem": pltpu.SemaphoreType.DMA((sems,)),
        "recv_sem": pltpu.SemaphoreType.DMA((sems,)),
        "local_sem": pltpu.SemaphoreType.DMA((16,)),
    }
    for q, order in enumerate(slab_orders):
        tile = (group_planes(modes, q), rows, det)
        scratch[f"packed{q}"] = pltpu.VMEM((2,) + slab_sizes + tile, f32)
        scratch[f"land0_{q}"] = pltpu.VMEM(slab_sizes + tile, f32)
        scratch[f"acc{q}"] = pltpu.VMEM(slab_sizes + tile, f32)
        scratch[f"landx{q}"] = pltpu.VMEM((more,) + tile, f32)
        scratch[f"full{q}"] = pltpu.VMEM((2,) + slab_sizes + (modes // groups, rows, det), f32)
        for step in range(3):
            kept = tuple(slab_sizes[i] for i in range(3) if i not in order[: step + 1])
            scratch[f"land{step + 1}_{q}"] = pltpu.VMEM((slab_sizes[order[step]] - 1,) + kept + tile, f32)
    for index, (i, j) in enumerate(directions()):
        shape = (det if i else block_rows, det if j else block_cols)
        scratch[f"num_slot{index}"] = pltpu.VMEM((2,) + shape, f32)
        scratch[f"light_slot{index}"] = pltpu.VMEM((1,) + shape, f32)
    names = ["offs", "probe_in", "patterns_in", "specimen_in"]
    names += [f"table_in{n}" for n in range(4)] + ["new_probe", "new_specimen"] + list(scratch)

    def kernel(*refs):
        update_kernel(extra, names, *refs)

    vmem = pl.BlockSpec(memory_space=pltpu.VMEM)
    return pl.pallas_call(
        kernel,
        name="update",
        out_shape=(
            jax.ShapeDtypeStruct(probe_modes.shape, f32),
            jax.ShapeDtypeStruct(specimen.shape, f32),
        ),
        in_specs=[pl.BlockSpec(memory_space=pltpu.SMEM)] + [pl.BlockSpec(memory_space=pl.ANY)] * 7,
        out_specs=(vmem, vmem),
        scratch_shapes=list(scratch.values()),
        compiler_params=pltpu.CompilerParams(has_side_effects=True, vmem_limit_bytes=56 * 1024 * 1024),
    )(offsets, probe_modes, patterns, specimen, *tables)


def solution(mesh):
    return jax.shard_map(
        body,
        mesh=mesh,
        in_specs=(
            P(),
            P(("scan", "tile"), None, None),
            P(None, "scan", "tile"),
            P(("scan", "tile"), None),
        ),
        out_specs=(P(), P(None, "scan", "tile")),
        check_vma=False,
    )
```

time: 99.6 us -> 92.4 us (0.928)
  local copies, waits for them, and re-layouts: 8.81 us -> 4.79 us
  Pallas kernels: 89.8 us -> 86.8 us
    unnamed x21 -> x5, local copies, waits for them, and re-layouts: 8.81 us -> 4.79 us
    pallas_call x3 -> x1, Pallas kernels: 89.8 us -> 86.8 us  [body(): pl.pallas_call(kernel, name='update', out_shape=(jax.ShapeDtypeStruct(pro...]
where the time goes in v2:
time: 92.4 us; the launch traced here: 92.2 us
  Pallas kernels  86.8 us (94%)
  local copies, waits for them, and re-layouts  4.79 us (5%)
    pallas_call x1, Pallas kernels, body(): pl.pallas_call(kernel, name='update', out_shape=(jax.ShapeDtypeStruct(pro...  86.8 us
    unnamed x5, local copies, waits for them, and re-layouts  4.79 us

profile of v2, /device:TPU:0, one launch (start us, length us, event | category | flops | bytes accessed | tf_op | source)
XLA Modules:
  0.0 92.2 jit_solution(13636736675237157009)
XLA Ops:
  0.6 1.3 %copy.10.refs_0_ = s32[4,2]{1,0:T(4,128)} copy(s32[4,2]{0,1:T(2,128)} %param.11) | data formatting | bytes 64 | tf_op args[3]
  2.0 86.8 %update.1 = (f32[12,2,128,128]{3,2,1,0:T(8,128)}, f32[2,128,256]{2,1,0:T(8,128)}) custom-call(s32[4,2]{1,0:T(4,128)} %copy.10.refs_0_, f32[12,2,128,128]{3,2,1,0:T(8,128)} %refs_1_.1, f32[4,128,128]{2,1,0:T(8,128)} %refs_2_.1, f32[2,128,256]{2,1,0:T(8,128)} %refs_3_.1, bf16[768,256]{1,0:T(8,128)(2,1)} %constant.8.clone.refs_4_, ...), custom_call_target="tpu_custom_call" | custom-call | tf_op jit(solution)/shard_map/update/pallas_call | solution.py:790
  88.7 0.0 copy-start
  88.7 2.7 %copy.13 = f32[12,2,128,128]{3,2,1,0:T(8,128)} copy(f32[12,2,128,128]{3,2,1,0:T(8,128)} %get-tuple-element.4) | data formatting | bytes 3145728
  91.5 0.0 copy-done
  91.5 0.7 copy.14
Async XLA Ops:
  88.7 2.8 %copy-start = (f32[2,128,256]{2,1,0:T(8,128)S(1)}, f32[2,128,256]{2,1,0:T(8,128)}, u32[]{:S(2)}) copy-start(f32[2,128,256]{2,1,0:T(8,128)} %get-tuple-element.5) | copy-start | bytes 786436

commit v3 on v2

--- a/solution.py
+++ b/solution.py
@@ -47,10 +47,8 @@
 
 core_dim = ("scan", 1, 2)
 slab_dims = (("scan", 2, 2), ("tile", 1, 2), ("scan", 4, 4))
-slab_orders = ((0, 1, 2), (1, 2, 0), (2, 0, 1))
 slab_sizes = tuple(size for _, _, size in slab_dims)
 slab_count = math.prod(slab_sizes)
-groups = len(slab_orders)
 
 
 def extra_bits():
@@ -62,8 +60,8 @@
     return bits
 
 
-def group_planes(modes, q):
-    return modes // groups + (q == 0)
+def order_of(q):
+    return (1, 0, 2) if q % 2 else (0, 1, 2)
 
 
 def slab_coords(tile):
@@ -119,12 +117,8 @@
     ext, pads, frame_num, frame_light = r["ext"], r["pads"], r["frame_num"], r["frame_light"]
     deep, half, far, patch, factor, num = r["deep"], r["half"], r["far"], r["patch"], r["factor"], r["num"]
     power, light, totals, total_land = r["power"], r["light"], r["totals"], r["total_land"]
-    packed = [r[f"packed{q}"] for q in range(groups)]
-    land0 = [r[f"land0_{q}"] for q in range(groups)]
-    acc = [r[f"acc{q}"] for q in range(groups)]
-    land = [[r[f"land{s}_{q}"] for q in range(groups)] for s in (1, 2, 3)]
-    landx = [r[f"landx{q}"] for q in range(groups)]
-    full = [r[f"full{q}"] for q in range(groups)]
+    packed, land0, acc, full = r["packed"], r["land0"], r["acc"], r["full"]
+    land1, land2, land3, landx, land_all = r["land1"], r["land2"], r["land3"], r["landx"], r["land_all"]
     num_slots = [r[f"num_slot{i}"] for i in range(8)]
     light_slots = [r[f"light_slot{i}"] for i in range(8)]
     gram_out, gram_land, gram_x, interior = r["gram_out"], r["gram_land"], r["gram_x"], r["interior"]
@@ -137,8 +131,8 @@
     own_blocks = block_cols // det
     col_blocks = own_blocks + 2
     ext_rows = block_rows + 2 * det
-    per = modes // groups
-    pair = per // 2
+    groups = modes // 2
+    mode_order = [q + h * groups for q in range(groups) for h in range(2)]
     rows = det // slab_count
     planes = 2 * modes
     used = [0]
@@ -156,6 +150,24 @@
 
     def remote(src, dst, moves):
         return route(src, dst, peer(moves))
+
+    class Batch:
+        def __init__(self, whole):
+            self.whole = whole
+            self.n = used[0]
+            used[0] += 1
+
+        def make(self, src, dst, device):
+            return pltpu.make_async_remote_copy(
+                src_ref=src, dst_ref=dst, send_sem=send_sem.at[self.n], recv_sem=recv_sem.at[self.n],
+                device_id=device, device_id_type=pl.DeviceIdType.MESH,
+            )
+
+        def send(self, src, dst, moves):
+            self.make(src, dst, peer(moves)).start()
+
+        def wait(self):
+            self.make(self.whole, self.whole, peer([(core_dim, 1)])).wait()
 
     def shifted(i, j):
         return {
@@ -267,8 +279,7 @@
             ext[:, outer_block(j), outer_rows(-1), :] = blank
 
     zeros_into(pads)
-    for q in range(groups):
-        zeros_into(packed[q])
+    zeros_into(num)
     zeros_into(light)
 
     lanes = lax.broadcasted_iota(jnp.int32, (det, det), 1)
@@ -276,8 +287,8 @@
     col_base = here["tile"] * block_cols - det
 
     def place(p):
-        row = jnp.clip(offs[p, 0] - row_base, 0, block_rows + det)
-        col = jnp.clip(offs[p, 1] - col_base, 0, block_cols + det)
+        row = jnp.clip(offs[0, p] - row_base, 0, block_rows + det)
+        col = jnp.clip(offs[1, p] - col_base, 0, block_cols + det)
         block = col // det
         return row, col, block, col - block * det
 
@@ -416,8 +427,8 @@
         patch_light = patch_re * patch_re + patch_im * patch_im
         light[...] = light[...] + patch_light
         total = total + patch_light * power[...]
-        for k in range(modes):
-            at = pl.ds(k * det, det)
+        for n, k in enumerate(mode_order):
+            at = pl.ds(n * det, det)
             pr, pi = probe[k, 0], probe[k, 1]
             for c, value in enumerate((pr * patch_re - pi * patch_im, pr * patch_im + pi * patch_re)):
                 high, low = halves(value)
@@ -454,181 +465,227 @@
     totals[1] = jnp.sum(total.reshape(det // 8, 8, det), axis=0)
     spread_shape = slab_sizes + (rows, det)
     for h in range(2):
-        packed[0][h, :, :, :, per] = light[...].reshape(spread_shape)
-
-    def spot_of(q, known, last=None):
+        r["packed_light"][h, :, :, :, 0] = light[...].reshape(spread_shape)
+
+    home = tuple(mine)
+
+    def spot_of(order, known, d=0):
         spot = [slice(None)] * 3
         for n in range(known):
-            spot[slab_orders[q][n]] = mine[slab_orders[q][n]]
-        if last is not None:
-            spot[slab_orders[q][known]] = last
+            spot[order[n]] = mine[order[n]]
+        if d:
+            i = order[known]
+            spot[i] = flipped(mine[i], slab_sizes[i], d)
         return tuple(spot)
 
-    def other(q, step, d):
-        i = slab_orders[q][step]
-        return flipped(mine[i], slab_sizes[i], d)
-
-    def reach(q, step):
-        return slab_dims[slab_orders[q][step]]
-
-    swap = [remote(packed[q].at[1 - core], land0[q], [(core_dim, 1)]) for q in range(groups)]
+    class Sum:
+        def __init__(self, order, direct, source, land0, acc, lands, landx):
+            self.order, self.direct, self.source, self.acc = order, direct, source, acc
+            self.land0, self.lands, self.landx = land0, lands, landx
+            self.swap = remote(source.at[1 - core], land0, [(core_dim, 1)])
+            self.batches = [Batch(land) for land in lands]
+
+        def send(self, step):
+            batch, land = self.batches[step], self.lands[step]
+            if self.direct:
+                for slot in range(1, slab_count):
+                    flips = slab_coords(slot)
+                    spot = tuple(flipped(mine[i], slab_sizes[i], flips[i]) for i in range(3))
+                    batch.send(self.acc.at[spot], land.at[slot - 1], list(zip(slab_dims, flips)))
+                return
+            dim = slab_dims[self.order[step]]
+            for d in range(1, dim[2]):
+                batch.send(self.acc.at[spot_of(self.order, step, d)], land.at[d - 1], [(dim, d)])
+
+        def swapped(self):
+            self.swap.wait()
+            self.acc[...] = self.source[core] + self.land0[...]
+            self.send(0)
+
+        def reduced(self, step):
+            self.batches[step].wait()
+            land = self.lands[step]
+            last = step == len(self.lands) - 1
+            spot = home if last else spot_of(self.order, step + 1)
+            value = self.acc[spot]
+            for d in range(land.shape[0]):
+                value = value + land[d]
+            self.acc[spot] = value
+            if not last:
+                self.send(step + 1)
+                return
+            for e, dim in enumerate(extra):
+                item = remote(self.acc.at[home], self.landx.at[e], [(dim, 1)])
+                item.start()
+                item.wait()
+                self.acc[home] = self.acc[home] + self.landx[e]
+
+    light_sum = Sum(
+        order_of(1), False, r["packed_light"], r["land0_light"], r["acc_light"],
+        [r["land1_light"], r["land2_light"], r["land3_light"]], r["landx_light"],
+    )
+    sums = []
+    for q in range(groups):
+        direct = q == groups - 1
+        lands = [land_all] if direct else [land1.at[q], land2.at[q], land3.at[q]]
+        sums.append(Sum(order_of(q), direct, packed.at[q], land0.at[q], acc.at[q], lands, landx.at[q]))
     total_swap = remote(totals, total_land, [(core_dim, 1)])
-    reducing = []
-    for q in range(groups):
-        reducing.append([])
-        for step in range(3):
-            dim = reach(q, step)
-            reducing[q].append(
-                [
-                    remote(acc[q].at[spot_of(q, step, other(q, step, d))], land[step][q].at[d - 1], [(dim, d)])
-                    for d in range(1, dim[2])
-                ]
-            )
-
-    def swap_end(q):
-        swap[q].wait()
-        acc[q][...] = packed[q][core] + land0[q][...]
-        launch(reducing[q][0])
-
-    def reduce_end(q, step):
-        settle(reducing[q][step])
-        spot = spot_of(q, step + 1)
-        value = acc[q][spot]
-        for d in range(1, reach(q, step)[2]):
-            value = value + land[step][q][d - 1]
-        acc[q][spot] = value
-        if step < 2:
-            launch(reducing[q][step + 1])
-
-    def backward(q, events):
-        def one(p, carry):
-            for when, event in events:
-                @pl.when(p == when)
-                def _():
-                    event()
-
+
+    def at_group(n):
+        if n == 0:
+            light_sum.swap.start()
+            total_swap.start()
+            return
+        sums[n - 1].swap.start()
+        if n == 1:
+            light_sum.swapped()
+        if n >= 2:
+            sums[n - 2].swapped()
+        if n == 3:
+            light_sum.reduced(0)
+        if n >= 4:
+            sums[n - 4].reduced(0)
+        if n == 5:
+            light_sum.reduced(1)
+        if n >= 6:
+            sums[n - 6].reduced(1)
+
+    def backward(q, carry):
+        for n in range(groups):
+            @pl.when(q == n)
+            def _():
+                at_group(n)
+
+        columns = pl.ds(pl.multiple_of(q * 2 * det, 2 * det), 2 * det)
+        for p in range(count):
             wide = jnp.concatenate([factor[p], factor[p]], axis=1)
             wide = jnp.concatenate([wide, wide], axis=0)
-            chosen = [h * (modes // 2) + q * pair + m for h in range(2) for m in range(pair)]
-            for n in range(0, per, 2):
-                high, low = halves(far[p, :, pl.ds(chosen[n] * det, 2 * det)] * wide)
-                stacked = jnp.concatenate([high, high, low], axis=0)
-                out = jnp.dot(left_b[...], stacked, preferred_element_type=f32)
-                high, low = halves(out)
-                for m in range(2):
-                    at = pl.ds((n + m) * det, det)
-                    for c in range(2):
-                        part_h = high[c * det : (c + 1) * det, m * det : (m + 1) * det]
-                        part_l = low[c * det : (c + 1) * det, m * det : (m + 1) * det]
-                        deep[at, pl.ds(c * det, det)] = part_h
-                        deep[at, pl.ds((2 + c) * det, det)] = part_h
-                        deep[at, pl.ds((4 + c) * det, det)] = part_l
-            some = pl.ds(0, per * det)
-            half[some, :] = jnp.dot(deep[some, :], right_b[...], preferred_element_type=f32)
-            patch_re, patch_im = patch[p, 0], patch[p, 1]
-            num_re = jnp.zeros((det, det), f32)
-            num_im = jnp.zeros((det, det), f32)
-            for n, k in enumerate(chosen):
-                at = pl.ds(n * det, det)
+            high, low = halves(far[p, :, columns] * wide)
+            stacked = jnp.concatenate([high, high, low], axis=0)
+            out = jnp.dot(left_b[...], stacked, preferred_element_type=f32)
+            high, low = halves(out)
+            for m in range(2):
+                at = pl.ds((2 * p + m) * det, det)
+                for c in range(2):
+                    part_h = high[c * det : (c + 1) * det, m * det : (m + 1) * det]
+                    part_l = low[c * det : (c + 1) * det, m * det : (m + 1) * det]
+                    deep[at, pl.ds(c * det, det)] = part_h
+                    deep[at, pl.ds((2 + c) * det, det)] = part_h
+                    deep[at, pl.ds((4 + c) * det, det)] = part_l
+        some = pl.ds(0, 2 * count * det)
+        half[some, :] = jnp.dot(deep[some, :], right_b[...], preferred_element_type=f32)
+        for m in range(2):
+            pr, pi = probe[q + m * groups, 0], probe[q + m * groups, 1]
+            grad_re = jnp.zeros((det, det), f32)
+            grad_im = jnp.zeros((det, det), f32)
+            for p in range(count):
+                at = pl.ds((2 * p + m) * det, det)
                 cr, ci = half[at, :det], half[at, det:]
-                pr, pi = probe[k, 0], probe[k, 1]
-                h, i = n // pair, n % pair
-                for c, value in enumerate((patch_re * cr + patch_im * ci, patch_re * ci - patch_im * cr)):
-                    spot = (h, slice(None), slice(None), slice(None), 2 * i + c)
-                    packed[q][spot] = packed[q][spot] + value.reshape(spread_shape)
-                num_re = num_re + pr * cr + pi * ci
-                num_im = num_im + pr * ci - pi * cr
-            if q:
-                num_re = num_re + num[p, 0]
-                num_im = num_im + num[p, 1]
-            if q < groups - 1:
-                num[p, 0] = num_re
-                num[p, 1] = num_im
-            else:
-                shift = place(p)[3]
-                pads[p, 0, pad_at, :] = pltpu.roll(num_re, shift, 1)
-                pads[p, 1, pad_at, :] = pltpu.roll(num_im, shift, 1)
-            return carry
-
-        lax.fori_loop(0, count, one, 0)
-
-    backward(0, [])
-    swap[0].start()
-    total_swap.start()
-    backward(1, [(2, lambda: swap_end(0))])
-    swap[1].start()
-    backward(2, [(2, lambda: (swap_end(1), reduce_end(0, 0)))])
-    swap[2].start()
-    build_frame(frame_num, 2)
-    num_fold = fold_copies(frame_num, num_slots)
-    reduce_end(0, 1)
-    swap_end(2)
-    fold_start(num_fold, (0, 1))
-    reduce_end(1, 0)
-    reduce_end(0, 2)
-    fold_start(num_fold, (2, 3))
-    reduce_end(1, 1)
-    reduce_end(2, 0)
-    fold_start(num_fold, (4, 5, 6, 7))
+                patch_re, patch_im = patch[p, 0], patch[p, 1]
+                grad_re = grad_re + patch_re * cr + patch_im * ci
+                grad_im = grad_im + patch_re * ci - patch_im * cr
+                num[p, 0] = num[p, 0] + (pr * cr + pi * ci)
+                num[p, 1] = num[p, 1] + (pr * ci - pi * cr)
+            packed[q, m, :, :, :, 0] = grad_re.reshape(spread_shape)
+            packed[q, m, :, :, :, 1] = grad_im.reshape(spread_shape)
+        return carry
+
+    lax.fori_loop(0, groups, backward, 0)
 
     tile = mine[0]
     for i in range(1, 3):
         tile = tile * slab_sizes[i] + mine[i]
     strip = pl.ds(pl.multiple_of(tile * rows, rows), rows)
-    home = tuple(mine)
-    own = [remote(full[q].at[(core,) + home], full[q].at[(core,) + home], [(core_dim, 1)]) for q in range(groups)]
-    gathering, passing = [], []
-    for q in range(groups):
-        gathering.append([])
-        passing.append([])
-        for step in range(3):
-            dim = reach(q, step)
-            spot = (core,) + spot_of(q, step + 1)
-            gathering[q].append(
-                [remote(full[q].at[spot], full[q].at[spot], [(dim, d)]) for d in range(1, dim[2])]
-            )
-            passed = []
+    own = Batch(full.at[(slice(None), core) + home])
+
+    class Gather:
+        def __init__(self, q):
+            self.q, self.order = q, order_of(q)
+            self.direct = q >= groups - 2
+            self.view = full.at[q, core]
+            if self.direct:
+                self.batches = [Batch(land_all)]
+            else:
+                wholes = [self.view.at[home[:2] + (pl.ds(0, slab_sizes[2] - 1),)]]
+                wholes += [self.view.at[spot_of(self.order, known)] for known in (2, 1)]
+                self.batches = [Batch(whole) for whole in wholes]
+            self.passing = Batch(land_all)
+
+        def both(self, batch, spot, moves):
+            batch.send(self.view.at[spot], self.view.at[spot], moves)
+
+        def hand(self, known):
+            for d in range(1, slab_sizes[self.order[known]]):
+                self.both(self.passing, spot_of(self.order, known, d), [(core_dim, 1)])
+
+        def send(self, step):
+            known = 3 - step
+            dim = slab_dims[self.order[known - 1]]
             for d in range(1, dim[2]):
-                spot = (core,) + spot_of(q, step, other(q, step, d))
-                passed.append(remote(full[q].at[spot], full[q].at[spot], [(core_dim, 1)]))
-            passing[q].append(passed)
-
-    def update_slab(q):
-        for e, dim in enumerate(extra):
-            item = remote(acc[q].at[home], landx[q].at[e], [(dim, 1)])
-            item.start()
-            item.wait()
-            acc[q][home] = acc[q][home] + landx[q][e]
-        scale = 1.0 / (acc[0][home + (per,)] + probe_reg)
-        for i in range(per):
-            k = core * (modes // 2) + q * pair + i // 2
-            full[q][(core,) + home + (i,)] = probe[k, i % 2, strip, :] + acc[q][home + (i,)] * scale
-        own[q].start()
-        launch(gathering[q][2])
-
-    def gather_end(q, step):
-        settle(gathering[q][step])
-        if step:
-            launch(gathering[q][step - 1])
-        launch(passing[q][step])
-
-    update_slab(0)
-    reduce_end(1, 2)
-    update_slab(1)
-    reduce_end(2, 1)
-    gather_end(0, 2)
-    reduce_end(2, 2)
-    update_slab(2)
-    gather_end(1, 2)
-    gather_end(0, 1)
+                self.both(self.batches[step], spot_of(self.order, known), [(dim, d)])
+
+        def begin(self):
+            q = self.q
+            for c in range(2):
+                value = probe[core * groups + q, c, strip, :] + acc[(q,) + home + (c,)] * scale
+                full[(q, core) + home + (c,)] = value
+            self.both(own, home, [(core_dim, 1)])
+            if self.direct:
+                for slot in range(1, slab_count):
+                    self.both(self.batches[0], home, list(zip(slab_dims, slab_coords(slot))))
+            else:
+                self.send(0)
+
+        def got(self, step):
+            self.batches[step].wait()
+            if self.direct:
+                for known in range(3):
+                    self.hand(known)
+                return
+            if step < 2:
+                self.send(step + 1)
+            self.hand(2 - step)
+
+    gathers = [Gather(q) for q in range(groups)]
+
+    at_group(groups)
+    for p in range(count):
+        shift = place(p)[3]
+        for c in range(2):
+            pads[p, c, pad_at, :] = pltpu.roll(num[p, c], shift, 1)
+    build_frame(frame_num, 2)
+    num_fold = fold_copies(frame_num, num_slots)
+    sums[5].swapped()
+    sums[1].reduced(1)
+    light_sum.reduced(2)
+    scale = 1.0 / (r["acc_light"][home + (0,)] + probe_reg)
+    sums[3].reduced(0)
+    fold_start(num_fold, range(8))
+    sums[2].reduced(1)
+    sums[4].reduced(0)
+    sums[0].reduced(2)
+    gathers[0].begin()
+    sums[3].reduced(1)
+    sums[1].reduced(2)
+    gathers[1].begin()
+    sums[4].reduced(1)
+    sums[2].reduced(2)
+    gathers[2].begin()
+    gathers[0].got(0)
+    sums[3].reduced(2)
+    gathers[3].begin()
+    sums[5].reduced(0)
+    gathers[5].begin()
+    sums[4].reduced(2)
+    gathers[4].begin()
+    gathers[1].got(0)
+    gathers[0].got(1)
 
     def slab_rows(spot):
         values = []
         for n in range(planes):
             c, k = n // modes, n % modes
-            h, rest = k // (modes // 2), k % (modes // 2)
-            q, m = rest // pair, rest % pair
-            values.append(full[q][(h,) + spot + (2 * m + c,)])
+            values.append(full[(k % groups, k // groups) + spot + (c,)])
         return jnp.concatenate(values, axis=0)
 
     tall = planes * rows
@@ -642,7 +699,7 @@
     entry = lax.broadcasted_iota(jnp.int32, (tall, det), 0)
     settled = jnp.where((entry >= plane) & (entry < plane + rows), 1.0, 0.0).astype(f32)
 
-    settle(own)
+    own.wait()
     held = slab_rows(home)
     turned = jnp.concatenate([-held[tall // 2 :], held[: tall // 2]], axis=0)
     wide = jnp.concatenate([held, turned], axis=1)
@@ -651,25 +708,27 @@
     )
     gram = full_dot(full_dot(pick, pairs * same), settled)
     total_swap.wait()
-    sums = [jnp.sum(totals[i] + total_land[i]) for i in range(2)]
+    both = [jnp.sum(totals[i] + total_land[i]) for i in range(2)]
     sheet_lanes = lax.broadcasted_iota(jnp.int32, (8, det), 1)
     first = lax.broadcasted_iota(jnp.int32, (8, det), 0) == 0
     at_measured = first & (sheet_lanes == det - 2)
     at_modelled = first & (sheet_lanes == det - 1)
-    sheet = jnp.where(at_measured, sums[0], jnp.where(at_modelled, sums[1], 0.0))
+    sheet = jnp.where(at_measured, both[0], jnp.where(at_modelled, both[1], 0.0))
     for part in range(planes // 8):
         piece = gram[part * 8 : (part + 1) * 8]
         sheet = sheet + (pltpu.roll(piece, part * 32, 1) if part else piece)
     gram_out[...] = sheet
-    spread = []
+    spread = Batch(gram_land)
     for slot in range(1, slab_count):
-        moves = list(zip(slab_dims, slab_coords(slot)))
-        spread.append(remote(gram_out, gram_land.at[slot - 1], moves))
-    launch(spread)
-    gather_end(2, 2)
-    gather_end(1, 1)
-    gather_end(2, 1)
-    settle(spread)
+        spread.send(gram_out, gram_land.at[slot - 1], list(zip(slab_dims, slab_coords(slot))))
+    gathers[2].got(0)
+    gathers[1].got(1)
+    gathers[3].got(0)
+    gathers[2].got(1)
+    gathers[0].got(2)
+    gathers[3].got(1)
+    gathers[1].got(2)
+    spread.wait()
     sheet = gram_out[...]
     for i in range(slab_count - 1):
         sheet = sheet + gram_land[i]
@@ -702,8 +761,10 @@
     )
     high, low = halves(mix * same)
     mixer = jnp.concatenate([high, low, high], axis=1)
-    for q in range(groups):
-        gather_end(q, 0)
+    gathers[2].got(2)
+    gathers[5].got(0)
+    gathers[4].got(0)
+    gathers[3].got(2)
 
     interior[0:2] = frame_num[:, det : det + block_rows, det : det + block_cols]
     interior[2] = frame_light[0, det : det + block_rows, det : det + block_cols]
@@ -711,9 +772,8 @@
     fold_end(num_fold, num_slots, slice(0, 2))
     new_specimen[...] = specimen[...] + interior[0:2] / (interior[2] + object_reg)[None]
 
-    for q in range(groups):
-        for step in range(3):
-            settle(passing[q][step])
+    for item in gathers:
+        item.passing.wait()
     for t in range(0, slab_count, 2):
         sides = [slab_rows(slab_coords(s)) for s in (t, t + 1)]
         high, low = halves(jnp.concatenate(sides, axis=1))
@@ -736,9 +796,10 @@
     extra = extra_bits()
     more = max(len(extra), 1)
     rows = det // slab_count
+    groups = modes // 2
     bf16 = jnp.bfloat16
     tables = [jnp.asarray(t) for t in dft_tables(det)]
-    sems = 160 + 6 * more
+    sems = 84 + (groups + 2) * len(extra)
     scratch = {
         "probe": pltpu.VMEM(probe_modes.shape, f32),
         "patterns": pltpu.VMEM(patterns.shape, f32),
@@ -766,16 +827,17 @@
         "recv_sem": pltpu.SemaphoreType.DMA((sems,)),
         "local_sem": pltpu.SemaphoreType.DMA((16,)),
     }
-    for q, order in enumerate(slab_orders):
-        tile = (group_planes(modes, q), rows, det)
-        scratch[f"packed{q}"] = pltpu.VMEM((2,) + slab_sizes + tile, f32)
-        scratch[f"land0_{q}"] = pltpu.VMEM(slab_sizes + tile, f32)
-        scratch[f"acc{q}"] = pltpu.VMEM(slab_sizes + tile, f32)
-        scratch[f"landx{q}"] = pltpu.VMEM((more,) + tile, f32)
-        scratch[f"full{q}"] = pltpu.VMEM((2,) + slab_sizes + (modes // groups, rows, det), f32)
-        for step in range(3):
-            kept = tuple(slab_sizes[i] for i in range(3) if i not in order[: step + 1])
-            scratch[f"land{step + 1}_{q}"] = pltpu.VMEM((slab_sizes[order[step]] - 1,) + kept + tile, f32)
+    for end, lead, planes in (("", (groups,), 2), ("_light", (), 1)):
+        tile = (planes, rows, det)
+        scratch["packed" + end] = pltpu.VMEM(lead + (2,) + slab_sizes + tile, f32)
+        scratch["land0" + end] = pltpu.VMEM(lead + slab_sizes + tile, f32)
+        scratch["acc" + end] = pltpu.VMEM(lead + slab_sizes + tile, f32)
+        scratch["land1" + end] = pltpu.VMEM(lead + (1, 2, slab_sizes[2]) + tile, f32)
+        scratch["land2" + end] = pltpu.VMEM(lead + (1, slab_sizes[2]) + tile, f32)
+        scratch["land3" + end] = pltpu.VMEM(lead + (slab_sizes[2] - 1,) + tile, f32)
+        scratch["landx" + end] = pltpu.VMEM(lead + (more,) + tile, f32)
+    scratch["land_all"] = pltpu.VMEM((slab_count - 1, 2, rows, det), f32)
+    scratch["full"] = pltpu.VMEM((groups, 2) + slab_sizes + (2, rows, det), f32)
     for index, (i, j) in enumerate(directions()):
         shape = (det if i else block_rows, det if j else block_cols)
         scratch[f"num_slot{index}"] = pltpu.VMEM((2,) + shape, f32)
@@ -798,7 +860,7 @@
         out_specs=(vmem, vmem),
         scratch_shapes=list(scratch.values()),
         compiler_params=pltpu.CompilerParams(has_side_effects=True, vmem_limit_bytes=56 * 1024 * 1024),
-    )(offsets, probe_modes, patterns, specimen, *tables)
+    )(offsets.T, probe_modes, patterns, specimen, *tables)
 
 
 def solution(mesh):

time: 92.4 us -> 79.7 us (0.86)
  Pallas kernels: 86.8 us -> 75.5 us
  local copies, waits for them, and re-layouts: 4.79 us -> 3.45 us
    pallas_call x1, Pallas kernels: 86.8 us -> 75.5 us  [body(): pl.pallas_call(kernel, name='update', out_shape=(jax.ShapeDtypeStruct(pro...]
    unnamed x5 -> x4, local copies, waits for them, and re-layouts: 4.79 us -> 3.45 us
where the time goes in v3:
time: 79.7 us; the launch traced here: 79.6 us
  Pallas kernels  75.5 us (95%)
  local copies, waits for them, and re-layouts  3.45 us (4%)
    pallas_call x1, Pallas kernels, body(): pl.pallas_call(kernel, name='update', out_shape=(jax.ShapeDtypeStruct(pro...  75.5 us
    unnamed x4, local copies, waits for them, and re-layouts  3.45 us

profile of v3, /device:TPU:0, one launch (start us, length us, event | category | flops | bytes accessed | tf_op | source)
XLA Modules:
  0.0 79.6 jit_solution(14373440263921346164)
XLA Ops:
  0.6 75.5 %update.1 = (f32[12,2,128,128]{3,2,1,0:T(8,128)}, f32[2,128,256]{2,1,0:T(8,128)}) custom-call(s32[2,4]{1,0:T(2,128)} %bitcast.1, f32[12,2,128,128]{3,2,1,0:T(8,128)} %refs_1_.1, f32[4,128,128]{2,1,0:T(8,128)} %refs_2_.1, f32[2,128,256]{2,1,0:T(8,128)} %refs_3_.1, bf16[768,256]{1,0:T(8,128)(2,1)} %constant.8.clone.refs_4_, ...), custom_call_target="tpu_custom_call" | custom-call | tf_op jit(solution)/shard_map/update/pallas_call | solution.py:852
  76.1 0.0 copy-start
  76.1 2.7 %copy.12 = f32[12,2,128,128]{3,2,1,0:T(8,128)} copy(f32[12,2,128,128]{3,2,1,0:T(8,128)} %get-tuple-element.4) | data formatting | bytes 3145728
  78.9 0.0 copy-done
  78.9 0.7 copy.13
Async XLA Ops:
  76.1 2.8 %copy-start = (f32[2,128,256]{2,1,0:T(8,128)S(1)}, f32[2,128,256]{2,1,0:T(8,128)}, u32[]{:S(2)}) copy-start(f32[2,128,256]{2,1,0:T(8,128)} %get-tuple-element.5) | copy-start | bytes 786436

commit v4 on v3

--- a/solution.py
+++ b/solution.py
@@ -60,10 +60,6 @@
     return bits
 
 
-def order_of(q):
-    return (1, 0, 2) if q % 2 else (0, 1, 2)
-
-
 def slab_coords(tile):
     coords = []
     for size in reversed(slab_sizes):
@@ -118,7 +114,7 @@
     deep, half, far, patch, factor, num = r["deep"], r["half"], r["far"], r["patch"], r["factor"], r["num"]
     power, light, totals, total_land = r["power"], r["light"], r["totals"], r["total_land"]
     packed, land0, acc, full = r["packed"], r["land0"], r["acc"], r["full"]
-    land1, land2, land3, landx, land_all = r["land1"], r["land2"], r["land3"], r["landx"], r["land_all"]
+    land1, land2, landx, land_all = r["land1"], r["land2"], r["landx"], r["land_all"]
     num_slots = [r[f"num_slot{i}"] for i in range(8)]
     light_slots = [r[f"light_slot{i}"] for i in range(8)]
     gram_out, gram_land, gram_x, interior = r["gram_out"], r["gram_land"], r["gram_x"], r["interior"]
@@ -132,7 +128,9 @@
     col_blocks = own_blocks + 2
     ext_rows = block_rows + 2 * det
     groups = modes // 2
-    mode_order = [q + h * groups for q in range(groups) for h in range(2)]
+    direct_sums = (groups - 1,)
+    direct_gathers = (groups - 1,)
+    fold_pieces = 2
     rows = det // slab_count
     planes = 2 * modes
     used = [0]
@@ -206,8 +204,10 @@
         return 0 if j == 1 else own_blocks + 1
 
     off_valid = valid(off_shift, 0)
-    edges = sorted({0, own_blocks - 1})
-    inner_blocks = [b for b in range(own_blocks) if b not in edges]
+    right_valid, left_valid = valid(0, 1), valid(0, -1)
+    near = jnp.where(right_valid, own_blocks - 1, 0)
+    distant = own_blocks - 1 - near
+    inner_blocks = list(range(1, own_blocks - 1))
     local = []
 
     def load(src, dst):
@@ -216,24 +216,22 @@
         local.append(item)
         return item
 
-    def row_copies(i, blocks):
-        copies = []
-        for b in blocks:
-            copies.append(
-                route(
-                    specimen_in.at[:, edge_rows(i, 0), b * det : (b + 1) * det],
-                    ext.at[:, 1 + b, outer_rows(i), :],
-                    shifted(i, 0),
-                )
-            )
-        return copies
-
-    off_rows = row_copies(off_shift, edges + inner_blocks)
-    on_rows = row_copies(on_shift, edges + inner_blocks)
+    def row_copy(i, b, c, channels):
+        channel = pl.ds(c, channels)
+        return route(
+            specimen_in.at[channel, edge_rows(i, 0), pl.ds(pl.multiple_of(b * det, det), det)],
+            ext.at[channel, 1 + b, outer_rows(i), :],
+            shifted(i, 0),
+        )
+
+    near_rows = [row_copy(off_shift, near, c, 1) for c in range(2)]
+    rest = [distant] * (own_blocks > 1) + inner_blocks
+    off_rows = [row_copy(off_shift, b, 0, 2) for b in rest]
+    on_rows = [row_copy(on_shift, b, 0, 2) for b in range(own_blocks)]
 
     @pl.when(off_valid)
     def _():
-        launch(off_rows[: len(edges)])
+        launch(near_rows)
 
     side = {}
     for j in (1, -1):
@@ -249,10 +247,9 @@
             side[j].start()
 
     launch(on_rows)
-    if inner_blocks:
-        @pl.when(off_valid)
-        def _():
-            launch(off_rows[len(edges) :])
+    @pl.when(off_valid)
+    def _():
+        launch(off_rows)
 
     probe_load = load(probe_in, probe)
     own_load = [
@@ -322,24 +319,30 @@
         pads[p, 0, pad_at, :] = pltpu.roll(power[...], place(p)[3], 1)
     build_frame(frame_light, 1)
 
-    @pl.when(off_valid)
-    def _():
-        for item in off_rows[: len(edges)]:
-            item.wait()
-
-    relay = []
-    for j in (1, -1):
-        b = edge_block(j)
-        item = route(
-            ext.at[:, 1 + b, outer_rows(-off_shift), :],
-            ext.at[:, outer_block(j), outer_rows(-off_shift), :],
+    def corner(j, c):
+        channel = pl.ds(c, 1)
+        return route(
+            ext.at[channel, 1 + edge_block(j), outer_rows(-off_shift), :],
+            ext.at[channel, outer_block(j), outer_rows(-off_shift), :],
             shifted(0, j),
         )
-        relay.append((item, off_valid & valid(0, j), off_valid & valid(0, -j)))
-
-        @pl.when(off_valid & valid(0, j))
+
+    relay = []
+    corners = {j: [corner(j, c) for c in range(2)] for j in (1, -1)}
+    for j in (1, -1):
+        relay += [(item, off_valid & valid(0, j), off_valid & valid(0, -j)) for item in corners[j]]
+    for c in range(2):
+        @pl.when(off_valid)
         def _():
-            item.start()
+            near_rows[c].wait()
+
+        @pl.when(off_valid & right_valid)
+        def _():
+            corners[1][c].start()
+
+        @pl.when(off_valid & left_valid & jnp.logical_not(right_valid))
+        def _():
+            corners[-1][c].start()
 
     for j in (1, -1):
         @pl.when(valid(0, j))
@@ -359,10 +362,15 @@
             item.start()
 
     settle(on_rows)
-    if inner_blocks:
-        @pl.when(off_valid)
-        def _():
-            settle(off_rows[len(edges) :])
+
+    @pl.when(off_valid)
+    def _():
+        settle(off_rows)
+
+    @pl.when(off_valid & left_valid & right_valid)
+    def _():
+        launch(corners[-1])
+
     for item, sent, came in relay:
         @pl.when(sent)
         def _():
@@ -382,64 +390,80 @@
         low = {-1: block - det, 0: 0, 1: 0}[shift]
         return pl.ds(low, block if shift == 0 else det)
 
-    def fold_copies(frame, slots):
-        copies = []
-        for index, (i, j) in enumerate(directions()):
-            copies.append(
-                route(frame.at[:, span(i, block_rows), span(j, block_cols)], slots[index], shifted(i, j))
-            )
-        return copies
-
-    def fold_start(copies, indices):
-        for index in indices:
-            @pl.when(valid(*directions()[index]))
-            def _():
-                copies[index].start()
-
-    def fold_end(copies, slots, into):
-        for index, (i, j) in enumerate(directions()):
-            @pl.when(valid(i, j))
-            def _():
-                copies[index].wait_send()
-
-            @pl.when(valid(-i, -j))
-            def _():
-                copies[index].wait_recv()
-                a, b = inner(i, block_rows), inner(j, block_cols)
-                interior[into, a, b] = interior[into, a, b] + slots[index][...]
-
-    light_fold = fold_copies(frame_light, light_slots)
-    fold_start(light_fold, range(8))
-
-    def forward(p, total):
+    class Fold:
+        def __init__(self, frame, slots, first):
+            self.slots, self.first = slots, first
+            self.batches = [Batch(slot) for slot in slots]
+            self.pending = []
+            channels = frame.shape[0]
+            for index in (0, 1, 4, 5, 6, 7, 2, 3):
+                i, j = directions()[index]
+                height = det if i else block_rows
+                low = span(i, block_rows).start
+                pieces = fold_pieces if j == 0 else 1
+                for c in range(channels):
+                    for n in range(pieces):
+                        size = height // pieces
+                        source = frame.at[pl.ds(c, 1), pl.ds(low + n * size, size), span(j, block_cols)]
+                        target = slots[index].at[pl.ds(c, 1), pl.ds(n * size, size)]
+                        self.pending.append((index, source, target))
+
+        def some(self, n):
+            for index, source, target in self.pending[:n]:
+                i, j = directions()[index]
+
+                @pl.when(valid(i, j))
+                def _():
+                    self.batches[index].make(source, target, shifted(i, j)).start()
+            self.pending = self.pending[n:]
+
+        def end(self):
+            into = slice(self.first, self.first + self.slots[0].shape[0])
+            for index, (i, j) in enumerate(directions()):
+                item = self.batches[index].make(self.slots[index], self.slots[index], shifted(i, j))
+
+                @pl.when(valid(i, j))
+                def _():
+                    item.wait_send()
+
+                @pl.when(valid(-i, -j))
+                def _():
+                    item.wait_recv()
+                    a, b = inner(i, block_rows), inner(j, block_cols)
+                    interior[into, a, b] = interior[into, a, b] + self.slots[index][...]
+
+    light_fold = Fold(frame_light, light_slots, 2)
+    light_fold.some(100)
+
+    total = jnp.zeros((det, det), f32)
+    for p in range(count):
         row, _, block, shift = place(p)
         back = lax.rem(det - shift, det)
-
-        def patch_part(c):
+        for c in range(2):
             first = pltpu.roll(ext[c, block, pl.ds(row, det), :], back, 1)
             second = pltpu.roll(ext[c, block + 1, pl.ds(row, det), :], back, 1)
-            return jnp.where(lanes < det - shift, first, second)
-
-        patch_re = patch_part(0)
-        patch_im = patch_part(1)
-        patch[p, 0] = patch_re
-        patch[p, 1] = patch_im
-        patch_light = patch_re * patch_re + patch_im * patch_im
+            patch[p, c] = jnp.where(lanes < det - shift, first, second)
+        patch_light = patch[p, 0] * patch[p, 0] + patch[p, 1] * patch[p, 1]
         light[...] = light[...] + patch_light
         total = total + patch_light * power[...]
-        for n, k in enumerate(mode_order):
-            at = pl.ds(n * det, det)
-            pr, pi = probe[k, 0], probe[k, 1]
-            for c, value in enumerate((pr * patch_re - pi * patch_im, pr * patch_im + pi * patch_re)):
-                high, low = halves(value)
-                deep[at, pl.ds(c * det, det)] = high
-                deep[at, pl.ds((2 + c) * det, det)] = high
-                deep[at, pl.ds((4 + c) * det, det)] = low
-        half[...] = jnp.dot(deep[...], right_f[...], preferred_element_type=f32)
-        model = jnp.zeros((det, det), f32)
-        for k in range(0, modes, 2):
-            lo_at, hi_at = pl.ds(k * det, det), pl.ds((k + 1) * det, det)
-            first, second = half[lo_at, :], half[hi_at, :]
+        factor[p] = jnp.zeros((det, det), f32)
+    some = pl.ds(0, 2 * count * det)
+
+    def forward(q, carry):
+        columns = pl.ds(pl.multiple_of(q * 2 * det, 2 * det), 2 * det)
+        for p in range(count):
+            patch_re, patch_im = patch[p, 0], patch[p, 1]
+            for m in range(2):
+                at = pl.ds((2 * p + m) * det, det)
+                pr, pi = probe[q + m * groups, 0], probe[q + m * groups, 1]
+                for c, value in enumerate((pr * patch_re - pi * patch_im, pr * patch_im + pi * patch_re)):
+                    high, low = halves(value)
+                    deep[at, pl.ds(c * det, det)] = high
+                    deep[at, pl.ds((2 + c) * det, det)] = high
+                    deep[at, pl.ds((4 + c) * det, det)] = low
+        half[some, :] = jnp.dot(deep[some, :], right_f[...], preferred_element_type=f32)
+        for p in range(count):
+            first, second = [half[pl.ds((2 * p + m) * det, det), :] for m in range(2)]
             paired = jnp.concatenate(
                 [
                     jnp.concatenate([first[:, :det], second[:, :det]], axis=1),
@@ -450,14 +474,15 @@
             high, low = halves(paired)
             stacked = jnp.concatenate([high, high, low], axis=0)
             out = jnp.dot(left_f[...], stacked, preferred_element_type=f32)
-            far[p, :, pl.ds(k * det, 2 * det)] = out
+            far[p, :, columns] = out
             squares = out * out
             both = squares[:det] + squares[det:]
-            model = model + both[:, :det] + both[:, det:]
-        factor[p] = jnp.sqrt(patterns[p]) / jnp.sqrt(jnp.maximum(model, light_floor)) - 1.0
-        return total
-
-    total = lax.fori_loop(0, count, forward, jnp.zeros((det, det), f32))
+            factor[p] = factor[p] + (both[:, :det] + both[:, det:])
+        return carry
+
+    lax.fori_loop(0, groups, forward, 0)
+    for p in range(count):
+        factor[p] = jnp.sqrt(patterns[p]) / jnp.sqrt(jnp.maximum(factor[p], light_floor)) - 1.0
     measured = jnp.zeros((det, det), f32)
     for p in range(count):
         measured = measured + patterns[p]
@@ -469,33 +494,34 @@
 
     home = tuple(mine)
 
-    def spot_of(order, known, d=0):
-        spot = [slice(None)] * 3
-        for n in range(known):
-            spot[order[n]] = mine[order[n]]
-        if d:
-            i = order[known]
-            spot[i] = flipped(mine[i], slab_sizes[i], d)
-        return tuple(spot)
+    def flips_of(stage):
+        flips = [()]
+        for i in range(3):
+            flips = [f + (d,) for f in flips for d in range(slab_sizes[i] if i in stage else 1)]
+        return flips[1:]
+
+    def spot_of(known, flips=(0, 0, 0)):
+        return tuple(flipped(mine[i], slab_sizes[i], flips[i]) if i in known else slice(None) for i in range(3))
+
+    def moves_of(flips):
+        return list(zip(slab_dims, flips))
+
+    two_steps, one_step = ((0, 1), (2,)), ((0, 1, 2),)
 
     class Sum:
-        def __init__(self, order, direct, source, land0, acc, lands, landx):
-            self.order, self.direct, self.source, self.acc = order, direct, source, acc
+        def __init__(self, stages, source, land0, acc, lands, landx):
+            self.stages, self.source, self.acc = stages, source, acc
             self.land0, self.lands, self.landx = land0, lands, landx
             self.swap = remote(source.at[1 - core], land0, [(core_dim, 1)])
             self.batches = [Batch(land) for land in lands]
 
+        def known(self, step):
+            return [i for stage in self.stages[: step + 1] for i in stage]
+
         def send(self, step):
-            batch, land = self.batches[step], self.lands[step]
-            if self.direct:
-                for slot in range(1, slab_count):
-                    flips = slab_coords(slot)
-                    spot = tuple(flipped(mine[i], slab_sizes[i], flips[i]) for i in range(3))
-                    batch.send(self.acc.at[spot], land.at[slot - 1], list(zip(slab_dims, flips)))
-                return
-            dim = slab_dims[self.order[step]]
-            for d in range(1, dim[2]):
-                batch.send(self.acc.at[spot_of(self.order, step, d)], land.at[d - 1], [(dim, d)])
+            for n, flips in enumerate(flips_of(self.stages[step])):
+                source = self.acc.at[spot_of(self.known(step), flips)]
+                self.batches[step].send(source, self.lands[step].at[n], moves_of(flips))
 
         def swapped(self):
             self.swap.wait()
@@ -505,13 +531,12 @@
         def reduced(self, step):
             self.batches[step].wait()
             land = self.lands[step]
-            last = step == len(self.lands) - 1
-            spot = home if last else spot_of(self.order, step + 1)
+            spot = spot_of(self.known(step))
             value = self.acc[spot]
             for d in range(land.shape[0]):
                 value = value + land[d]
             self.acc[spot] = value
-            if not last:
+            if step < len(self.lands) - 1:
                 self.send(step + 1)
                 return
             for e, dim in enumerate(extra):
@@ -521,14 +546,18 @@
                 self.acc[home] = self.acc[home] + self.landx[e]
 
     light_sum = Sum(
-        order_of(1), False, r["packed_light"], r["land0_light"], r["acc_light"],
-        [r["land1_light"], r["land2_light"], r["land3_light"]], r["landx_light"],
+        two_steps, r["packed_light"], r["land0_light"], r["acc_light"],
+        [r["land1_light"], r["land2_light"]], r["landx_light"],
     )
     sums = []
     for q in range(groups):
-        direct = q == groups - 1
-        lands = [land_all] if direct else [land1.at[q], land2.at[q], land3.at[q]]
-        sums.append(Sum(order_of(q), direct, packed.at[q], land0.at[q], acc.at[q], lands, landx.at[q]))
+        direct = q in direct_sums
+        sums.append(
+            Sum(
+                one_step if direct else two_steps, packed.at[q], land0.at[q], acc.at[q],
+                [land_all.at[q]] if direct else [land1.at[q], land2.at[q]], landx.at[q],
+            )
+        )
     total_swap = remote(totals, total_land, [(core_dim, 1)])
 
     def at_group(n):
@@ -537,18 +566,10 @@
             total_swap.start()
             return
         sums[n - 1].swap.start()
-        if n == 1:
+        if n == 2:
             light_sum.swapped()
-        if n >= 2:
-            sums[n - 2].swapped()
-        if n == 3:
-            light_sum.reduced(0)
-        if n >= 4:
-            sums[n - 4].reduced(0)
-        if n == 5:
-            light_sum.reduced(1)
-        if n >= 6:
-            sums[n - 6].reduced(1)
+        if n >= 3:
+            sums[n - 3].swapped()
 
     def backward(q, carry):
         for n in range(groups):
@@ -572,7 +593,6 @@
                     deep[at, pl.ds(c * det, det)] = part_h
                     deep[at, pl.ds((2 + c) * det, det)] = part_h
                     deep[at, pl.ds((4 + c) * det, det)] = part_l
-        some = pl.ds(0, 2 * count * det)
         half[some, :] = jnp.dot(deep[some, :], right_b[...], preferred_element_type=f32)
         for m in range(2):
             pr, pi = probe[q + m * groups, 0], probe[q + m * groups, 1]
@@ -600,29 +620,25 @@
 
     class Gather:
         def __init__(self, q):
-            self.q, self.order = q, order_of(q)
-            self.direct = q >= groups - 2
+            self.q = q
             self.view = full.at[q, core]
-            if self.direct:
-                self.batches = [Batch(land_all)]
+            if q in direct_gathers:
+                self.stages = one_step
+                self.batches = [Batch(land_all.at[0])]
             else:
-                wholes = [self.view.at[home[:2] + (pl.ds(0, slab_sizes[2] - 1),)]]
-                wholes += [self.view.at[spot_of(self.order, known)] for known in (2, 1)]
-                self.batches = [Batch(whole) for whole in wholes]
-            self.passing = Batch(land_all)
+                self.stages = two_steps[::-1]
+                self.batches = [Batch(land2.at[0]), Batch(land1.at[0])]
+            self.passing = Batch(land_all.at[0])
 
         def both(self, batch, spot, moves):
             batch.send(self.view.at[spot], self.view.at[spot], moves)
 
-        def hand(self, known):
-            for d in range(1, slab_sizes[self.order[known]]):
-                self.both(self.passing, spot_of(self.order, known, d), [(core_dim, 1)])
+        def left(self, step):
+            return [i for stage in self.stages[step:] for i in stage]
 
         def send(self, step):
-            known = 3 - step
-            dim = slab_dims[self.order[known - 1]]
-            for d in range(1, dim[2]):
-                self.both(self.batches[step], spot_of(self.order, known), [(dim, d)])
+            for flips in flips_of(self.stages[step]):
+                self.both(self.batches[step], spot_of(self.left(step)), moves_of(flips))
 
         def begin(self):
             q = self.q
@@ -630,21 +646,14 @@
                 value = probe[core * groups + q, c, strip, :] + acc[(q,) + home + (c,)] * scale
                 full[(q, core) + home + (c,)] = value
             self.both(own, home, [(core_dim, 1)])
-            if self.direct:
-                for slot in range(1, slab_count):
-                    self.both(self.batches[0], home, list(zip(slab_dims, slab_coords(slot))))
-            else:
-                self.send(0)
+            self.send(0)
 
         def got(self, step):
             self.batches[step].wait()
-            if self.direct:
-                for known in range(3):
-                    self.hand(known)
-                return
-            if step < 2:
+            if step < len(self.stages) - 1:
                 self.send(step + 1)
-            self.hand(2 - step)
+            for flips in flips_of(self.stages[step]):
+                self.both(self.passing, spot_of(self.left(step), flips), [(core_dim, 1)])
 
     gathers = [Gather(q) for q in range(groups)]
 
@@ -654,32 +663,23 @@
         for c in range(2):
             pads[p, c, pad_at, :] = pltpu.roll(num[p, c], shift, 1)
     build_frame(frame_num, 2)
-    num_fold = fold_copies(frame_num, num_slots)
-    sums[5].swapped()
-    sums[1].reduced(1)
-    light_sum.reduced(2)
+    sums[groups - 2].swapped()
+    sums[groups - 1].swapped()
+    light_sum.reduced(0)
+    num_fold = Fold(frame_num, num_slots, 0)
+    for q in range(groups - 1):
+        sums[q].reduced(0)
+        num_fold.some(2)
+    light_sum.reduced(1)
     scale = 1.0 / (r["acc_light"][home + (0,)] + probe_reg)
-    sums[3].reduced(0)
-    fold_start(num_fold, range(8))
-    sums[2].reduced(1)
-    sums[4].reduced(0)
-    sums[0].reduced(2)
-    gathers[0].begin()
-    sums[3].reduced(1)
-    sums[1].reduced(2)
-    gathers[1].begin()
-    sums[4].reduced(1)
-    sums[2].reduced(2)
-    gathers[2].begin()
-    gathers[0].got(0)
-    sums[3].reduced(2)
-    gathers[3].begin()
-    sums[5].reduced(0)
-    gathers[5].begin()
-    sums[4].reduced(2)
-    gathers[4].begin()
-    gathers[1].got(0)
-    gathers[0].got(1)
+    for q in range(groups):
+        if q not in direct_sums:
+            sums[q].reduced(1)
+            gathers[q].begin()
+            num_fold.some(2)
+    sums[groups - 1].reduced(0)
+    gathers[groups - 1].begin()
+    num_fold.some(2)
 
     def slab_rows(spot):
         values = []
@@ -721,13 +721,11 @@
     spread = Batch(gram_land)
     for slot in range(1, slab_count):
         spread.send(gram_out, gram_land.at[slot - 1], list(zip(slab_dims, slab_coords(slot))))
-    gathers[2].got(0)
-    gathers[1].got(1)
-    gathers[3].got(0)
-    gathers[2].got(1)
-    gathers[0].got(2)
-    gathers[3].got(1)
-    gathers[1].got(2)
+    for q in range(groups):
+        if q not in direct_gathers:
+            gathers[q].got(0)
+            num_fold.some(2)
+    num_fold.some(100)
     spread.wait()
     sheet = gram_out[...]
     for i in range(slab_count - 1):
@@ -761,15 +759,13 @@
     )
     high, low = halves(mix * same)
     mixer = jnp.concatenate([high, low, high], axis=1)
-    gathers[2].got(2)
-    gathers[5].got(0)
-    gathers[4].got(0)
-    gathers[3].got(2)
+    for q in range(groups):
+        gathers[q].got(0 if q in direct_gathers else 1)
 
     interior[0:2] = frame_num[:, det : det + block_rows, det : det + block_cols]
     interior[2] = frame_light[0, det : det + block_rows, det : det + block_cols]
-    fold_end(light_fold, light_slots, slice(2, 3))
-    fold_end(num_fold, num_slots, slice(0, 2))
+    light_fold.end()
+    num_fold.end()
     new_specimen[...] = specimen[...] + interior[0:2] / (interior[2] + object_reg)[None]
 
     for item in gathers:
@@ -809,8 +805,8 @@
         "pads": pltpu.VMEM((count, 2, 2 * (ext_rows - det) + det, det), f32),
         "frame_num": pltpu.VMEM((2, ext_rows, ext_cols), f32),
         "frame_light": pltpu.VMEM((1, ext_rows, ext_cols), f32),
-        "deep": pltpu.VMEM((modes * det, 6 * det), bf16),
-        "half": pltpu.VMEM((modes * det, 2 * det), f32),
+        "deep": pltpu.VMEM((2 * count * det, 6 * det), bf16),
+        "half": pltpu.VMEM((2 * count * det, 2 * det), f32),
         "far": pltpu.VMEM((count, 2 * det, modes * det), f32),
         "patch": pltpu.VMEM((count, 2, det, det), f32),
         "factor": pltpu.VMEM((count, det, det), f32),
@@ -832,11 +828,10 @@
         scratch["packed" + end] = pltpu.VMEM(lead + (2,) + slab_sizes + tile, f32)
         scratch["land0" + end] = pltpu.VMEM(lead + slab_sizes + tile, f32)
         scratch["acc" + end] = pltpu.VMEM(lead + slab_sizes + tile, f32)
-        scratch["land1" + end] = pltpu.VMEM(lead + (1, 2, slab_sizes[2]) + tile, f32)
-        scratch["land2" + end] = pltpu.VMEM(lead + (1, slab_sizes[2]) + tile, f32)
-        scratch["land3" + end] = pltpu.VMEM(lead + (slab_sizes[2] - 1,) + tile, f32)
+        scratch["land1" + end] = pltpu.VMEM(lead + (slab_sizes[0] * slab_sizes[1] - 1, slab_sizes[2]) + tile, f32)
+        scratch["land2" + end] = pltpu.VMEM(lead + (slab_sizes[2] - 1,) + tile, f32)
         scratch["landx" + end] = pltpu.VMEM(lead + (more,) + tile, f32)
-    scratch["land_all"] = pltpu.VMEM((slab_count - 1, 2, rows, det), f32)
+    scratch["land_all"] = pltpu.VMEM((groups, slab_count - 1, 2, rows, det), f32)
     scratch["full"] = pltpu.VMEM((groups, 2) + slab_sizes + (2, rows, det), f32)
     for index, (i, j) in enumerate(directions()):
         shape = (det if i else block_rows, det if j else block_cols)

time: 79.7 us -> 74.6 us (0.936)
  Pallas kernels: 75.5 us -> 70.4 us
    pallas_call x1, Pallas kernels: 75.5 us -> 70.4 us  [body(): pl.pallas_call(kernel, name='update', out_shape=(jax.ShapeDtypeStruct(pro...]
where the time goes in v4:
time: 74.6 us; the launch traced here: 74.5 us
  Pallas kernels  70.4 us (94%)
  local copies, waits for them, and re-layouts  3.45 us (5%)
    pallas_call x1, Pallas kernels, body(): pl.pallas_call(kernel, name='update', out_shape=(jax.ShapeDtypeStruct(pro...  70.4 us
    unnamed x4, local copies, waits for them, and re-layouts  3.45 us

profile of v4, /device:TPU:0, one launch (start us, length us, event | category | flops | bytes accessed | tf_op | source)
XLA Modules:
  0.0 74.5 jit_solution(13111522513000204987)
XLA Ops:
  0.6 70.4 %update.1 = (f32[12,2,128,128]{3,2,1,0:T(8,128)}, f32[2,128,256]{2,1,0:T(8,128)}) custom-call(s32[2,4]{1,0:T(2,128)} %bitcast.1, f32[12,2,128,128]{3,2,1,0:T(8,128)} %refs_1_.1, f32[4,128,128]{2,1,0:T(8,128)} %refs_2_.1, f32[2,128,256]{2,1,0:T(8,128)} %refs_3_.1, bf16[768,256]{1,0:T(8,128)(2,1)} %constant.8.clone.refs_4_, ...), custom_call_target="tpu_custom_call" | custom-call | tf_op jit(solution)/shard_map/update/pallas_call | solution.py:847
  71.0 0.0 copy-start
  71.0 2.7 %copy.12 = f32[12,2,128,128]{3,2,1,0:T(8,128)} copy(f32[12,2,128,128]{3,2,1,0:T(8,128)} %get-tuple-element.4) | data formatting | bytes 3145728
  73.8 0.0 copy-done
  73.8 0.7 copy.13
Async XLA Ops:
  71.0 2.8 %copy-start = (f32[2,128,256]{2,1,0:T(8,128)S(1)}, f32[2,128,256]{2,1,0:T(8,128)}, u32[]{:S(2)}) copy-start(f32[2,128,256]{2,1,0:T(8,128)} %get-tuple-element.5) | copy-start | bytes 786436

commit v5 on v4

--- a/solution.py
+++ b/solution.py
@@ -129,7 +129,7 @@
     ext_rows = block_rows + 2 * det
     groups = modes // 2
     direct_sums = (groups - 1,)
-    direct_gathers = (groups - 1,)
+    direct_gathers = ()
     fold_pieces = 2
     rows = det // slab_count
     planes = 2 * modes
@@ -675,10 +675,10 @@
     for q in range(groups):
         if q not in direct_sums:
             sums[q].reduced(1)
-            gathers[q].begin()
             num_fold.some(2)
     sums[groups - 1].reduced(0)
-    gathers[groups - 1].begin()
+    for q in range(groups):
+        gathers[q].begin()
     num_fold.some(2)
 
     def slab_rows(spot):
@@ -781,6 +781,48 @@
                 ]
 
 
+def emit_kernel(*refs):
+    sources, targets, held = refs[:2], refs[2:4], refs[4:6]
+    come, gone = refs[6:]
+    steps = []
+    for source, target, buffer in zip(sources, targets, held):
+        rows = max(source.shape[0] // 6, 1)
+        for low in range(0, source.shape[0], rows):
+            at = pl.ds(low, rows)
+            n = len(steps)
+            steps.append(
+                (
+                    pltpu.make_async_copy(source.at[at], buffer.at[at], come.at[n]),
+                    pltpu.make_async_copy(buffer.at[at], target.at[at], gone.at[n]),
+                )
+            )
+    for arrive, _ in steps:
+        arrive.start()
+    for arrive, leave in steps:
+        arrive.wait()
+        leave.start()
+    for _, leave in steps:
+        leave.wait()
+
+
+def emit(probe, specimen):
+    anywhere = pl.BlockSpec(memory_space=pl.ANY)
+    return pl.pallas_call(
+        emit_kernel,
+        name="emit",
+        out_shape=tuple(jax.ShapeDtypeStruct(x.shape, x.dtype) for x in (probe, specimen)),
+        in_specs=[anywhere] * 2,
+        out_specs=(anywhere,) * 2,
+        scratch_shapes=[
+            pltpu.VMEM(probe.shape, probe.dtype),
+            pltpu.VMEM(specimen.shape, specimen.dtype),
+            pltpu.SemaphoreType.DMA((16,)),
+            pltpu.SemaphoreType.DMA((16,)),
+        ],
+        compiler_params=pltpu.CompilerParams(vmem_limit_bytes=56 * 1024 * 1024),
+    )(probe, specimen)
+
+
 def body(probe_modes, patterns, specimen, offsets):
     f32 = jnp.float32
     modes, _, det, _ = probe_modes.shape
@@ -844,7 +886,7 @@
         update_kernel(extra, names, *refs)
 
     vmem = pl.BlockSpec(memory_space=pltpu.VMEM)
-    return pl.pallas_call(
+    results = pl.pallas_call(
         kernel,
         name="update",
         out_shape=(
@@ -856,6 +898,7 @@
         scratch_shapes=list(scratch.values()),
         compiler_params=pltpu.CompilerParams(has_side_effects=True, vmem_limit_bytes=56 * 1024 * 1024),
     )(offsets.T, probe_modes, patterns, specimen, *tables)
+    return emit(*results)
 
 
 def solution(mesh):

time: 74.6 us -> 72.4 us (0.971)
  local copies, waits for them, and re-layouts: 3.45 us -> 0 us
  Pallas kernels: 70.4 us -> 71.6 us
    unnamed x4 -> x0, local copies, waits for them, and re-layouts: 3.45 us -> none
    pallas_call x0 -> x1, Pallas kernels: none -> 2.45 us  [emit(): pl.pallas_call(emit_kernel, name='emit', out_shape=tuple((jax.ShapeDtypeS...]
    pallas_call x1, Pallas kernels: 70.4 us -> 69.2 us  [body(): pl.pallas_call(kernel, name='update', out_shape=(jax.ShapeDtypeStruct(pro...]
where the time goes in v5:
time: 72.4 us; the launch traced here: 72.2 us
  Pallas kernels  71.6 us (99%)
    pallas_call x1, Pallas kernels, body(): pl.pallas_call(kernel, name='update', out_shape=(jax.ShapeDtypeStruct(pro...  69.2 us
    pallas_call x1, Pallas kernels, emit(): pl.pallas_call(emit_kernel, name='emit', out_shape=tuple((jax.ShapeDtypeS...  2.45 us

profile of v5, /device:TPU:0, one launch (start us, length us, event | category | flops | bytes accessed | tf_op | source)
XLA Modules:
  0.0 72.2 jit_solution(13690905072922245685)
XLA Ops:
  0.6 69.2 %update.1 = (f32[12,2,128,128]{3,2,1,0:T(8,128)}, f32[2,128,256]{2,1,0:T(8,128)}) custom-call(s32[2,4]{1,0:T(2,128)} %bitcast.1, f32[12,2,128,128]{3,2,1,0:T(8,128)} %refs_1_.1, f32[4,128,128]{2,1,0:T(8,128)} %refs_2_.1, f32[2,128,256]{2,1,0:T(8,128)} %refs_3_.1, bf16[768,256]{1,0:T(8,128)(2,1)} %constant.8.clone.refs_4_, ...), custom_call_target="tpu_custom_call" | custom-call | tf_op jit(solution)/shard_map/update/pallas_call | solution.py:889
  69.8 2.4 %emit.1 = (f32[12,2,128,128]{3,2,1,0:T(8,128)}, f32[2,128,256]{2,1,0:T(8,128)}) custom-call(f32[12,2,128,128]{3,2,1,0:T(8,128)} %get-tuple-element.4.refs_0_, f32[2,128,256]{2,1,0:T(8,128)} %get-tuple-element.5.refs_1_), custom_call_target="tpu_custom_call" | custom-call | tf_op jit(solution)/shard_map/emit/pallas_call | solution.py:810

commit v6 on v5

--- a/solution.py
+++ b/solution.py
@@ -816,8 +816,8 @@
         scratch_shapes=[
             pltpu.VMEM(probe.shape, probe.dtype),
             pltpu.VMEM(specimen.shape, specimen.dtype),
-            pltpu.SemaphoreType.DMA((16,)),
-            pltpu.SemaphoreType.DMA((16,)),
+            pltpu.SemaphoreType.DMA((8,)),
+            pltpu.SemaphoreType.DMA((8,)),
         ],
         compiler_params=pltpu.CompilerParams(vmem_limit_bytes=56 * 1024 * 1024),
     )(probe, specimen)
@@ -837,7 +837,7 @@
     groups = modes // 2
     bf16 = jnp.bfloat16
     tables = [jnp.asarray(t) for t in dft_tables(det)]
-    sems = 84 + (groups + 2) * len(extra)
+    sems = 70 + (groups + 2) * len(extra)
     scratch = {
         "probe": pltpu.VMEM(probe_modes.shape, f32),
         "patterns": pltpu.VMEM(patterns.shape, f32),
@@ -863,7 +863,7 @@
         "interior": pltpu.VMEM((3, block_rows, block_cols), f32),
         "send_sem": pltpu.SemaphoreType.DMA((sems,)),
         "recv_sem": pltpu.SemaphoreType.DMA((sems,)),
-        "local_sem": pltpu.SemaphoreType.DMA((16,)),
+        "local_sem": pltpu.SemaphoreType.DMA((9,)),
     }
     for end, lead, planes in (("", (groups,), 2), ("_light", (), 1)):
         tile = (planes, rows, det)

time: 72.4 us -> 72 us (level)
  no operation moved by 1% of the time
where the time goes in v6:
time: 72 us; the launch traced here: 71.8 us
  Pallas kernels  71.2 us (99%)
    pallas_call x1, Pallas kernels, body(): pl.pallas_call(kernel, name='update', out_shape=(jax.ShapeDtypeStruct(pro...  68.9 us
    pallas_call x1, Pallas kernels, emit(): pl.pallas_call(emit_kernel, name='emit', out_shape=tuple((jax.ShapeDtypeS...  2.3 us

profile of v6, /device:TPU:0, one launch (start us, length us, event | category | flops | bytes accessed | tf_op | source)
XLA Modules:
  0.0 71.8 jit_solution(14719156502516060894)
XLA Ops:
  0.6 68.9 %update.1 = (f32[12,2,128,128]{3,2,1,0:T(8,128)}, f32[2,128,256]{2,1,0:T(8,128)}) custom-call(s32[2,4]{1,0:T(2,128)} %bitcast.1, f32[12,2,128,128]{3,2,1,0:T(8,128)} %refs_1_.1, f32[4,128,128]{2,1,0:T(8,128)} %refs_2_.1, f32[2,128,256]{2,1,0:T(8,128)} %refs_3_.1, bf16[768,256]{1,0:T(8,128)(2,1)} %constant.8.clone.refs_4_, ...), custom_call_target="tpu_custom_call" | custom-call | tf_op jit(solution)/shard_map/update/pallas_call | solution.py:889
  69.5 2.3 %emit.1 = (f32[12,2,128,128]{3,2,1,0:T(8,128)}, f32[2,128,256]{2,1,0:T(8,128)}) custom-call(f32[12,2,128,128]{3,2,1,0:T(8,128)} %get-tuple-element.4.refs_0_, f32[2,128,256]{2,1,0:T(8,128)} %get-tuple-element.5.refs_1_), custom_call_target="tpu_custom_call" | custom-call | tf_op jit(solution)/shard_map/emit/pallas_call | solution.py:810
